TPU v7x, 128 devices: a whole 4x4x4 slice. The times are simulated.
128 devices in a mesh: enc: 4 (over z_lo, core), fsdp: 32 (over z_hi, x, y).
Axes of the slice: x: 4, y: 4, z: 4 (z_hi: 2, z_lo: 2; z = z_hi * 2 + z_lo), core: 2. Of those that a mesh axis runs over, the one named last changes fastest.
Arguments:
- enc_features: bfloat16 [32, 8, 1024, 512], P(None, 'enc', 'fsdp'), may hold values from -6 to 6
- enc_gain: float32 [1, 512], replicated, may hold values from 0.1 to 1.9
- enc_kernel: bfloat16 [1, 3, 512, 512], replicated, may hold values from -0.15625 to 0.15625
- out_kernel: bfloat16 [512, 16], replicated, may hold values from -0.25 to 0.25
- clip_start: int32 [32], replicated, may hold values from 0 to 3
- assign: int32 [32], replicated, may hold values from 0 to 31, each once
- embed_weight: bfloat16 [3072, 64], P('fsdp'), may hold values from -0.75 to 0.75
- mod_shift: float32 [32, 3072], P('fsdp'), may hold values from -3 to 3
- mod_scale: float32 [32, 3072], P('fsdp'), may hold values from -3 to 3
- value_weight: bfloat16 [3072, 1536], P('fsdp'), may hold values from -0.109375 to 0.109375
- value_cotangent: bfloat16 [32, 8, 256, 1536], P('fsdp', 'enc'), may hold values from -6 to 6
Outputs:
- values: bfloat16 [32, 8, 256, 1536], P('fsdp', 'enc')
- grad_value: float32 [3072, 1536], P(('enc', 'fsdp'))
- grad_embed: float32 [3072, 64], P(('enc', 'fsdp'))
Inputs may be any that keep to these rules, and one draw needn't show every extreme that they name: Sample s is made from clip assign[s]; every clip is taken by exactly one sample.
All inputs are finite; a program needn't handle non-finite values.
Results may differ from a plain program's by a relative error of at most 0.025.
Values may be sent and summed in bfloat16 or wider, within the bound.
No kernel may reach another device: no remote copies, remote signals or barrier semaphores. Data moves between devices by JAX's collectives and lax.ppermute only.
A program may use at most 192 MiB of HBM per device.

v0:
```python
import jax
import jax.numpy as jnp
from jax import lax
from jax.sharding import PartitionSpec as P


def from_behind(x, axis, by):
    size = lax.axis_size(axis)
    pairs = [(i, i + by) for i in range(size) if 0 <= i + by < size]
    return lax.ppermute(x, axis, pairs)


def in_one_piece(arrays, axis, dim, along):
    widths = [a.shape[along] for a in arrays]
    both = jnp.concatenate(arrays, axis=along)
    out = lax.all_gather(both, axis, axis=dim, tiled=True)
    return tuple(jnp.split(out, [sum(widths[:k]) for k in range(1, len(widths))], axis=along))


def in_one_piece_2(arrays, axis, dim, along):
    both = jnp.concatenate(arrays, axis=along)
    out, at, gathered = (lax.psum_scatter(both, axis, scatter_dimension=dim, tiled=True), 0, [])
    for a in arrays:
        gathered.append(lax.slice_in_dim(out, at, at + a.shape[along], axis=along))
        at += a.shape[along]
    return tuple(gathered)


def channel_norm(activation, gain_row):
    scaling = lax.rsqrt(jnp.mean(activation * activation, axis=-1, keepdims=True) + 1e-06)
    return activation * scaling * gain_row


def local(
    enc_features,
    enc_gain,
    enc_kernel,
    out_kernel,
    clip_start,
    assign,
    embed_weight,
    mod_shift,
    mod_scale,
    value_weight,
    value_cotangent,
):
    clip_count, frame_count, pixel_count, channels = enc_features.shape
    first_frame = lax.axis_index("enc") * frame_count
    frame_ids = first_frame + jnp.arange(frame_count, dtype=jnp.int32)
    live_mask = (frame_ids[None, :] >= clip_start[:, None]).astype(jnp.float32)[:, :, None, None]
    stored = enc_features
    activation = stored.astype(jnp.float32)
    normed = (live_mask * channel_norm(activation, enc_gain[0])).astype(jnp.bfloat16)
    before = from_behind(normed, "enc", 1)
    padded = jnp.concatenate([before, normed], axis=1)
    convolved = jnp.zeros(activation.shape, jnp.float32)
    for offset in range(3):
        window = padded[:, offset : offset + frame_count].reshape(-1, channels)
        convolved = convolved + jnp.dot(
            window, enc_kernel[0, offset], preferred_element_type=jnp.float32
        ).reshape(activation.shape)
    stored = (activation + jax.nn.silu(convolved)).astype(jnp.bfloat16)
    latent = jnp.dot(stored.reshape(-1, channels), out_kernel, preferred_element_type=jnp.float32)
    latent = latent.reshape(clip_count, frame_count, pixel_count, out_kernel.shape[1])
    latent = (latent * live_mask).astype(jnp.bfloat16)
    latent = latent.reshape(clip_count, frame_count, pixel_count // 4, 4 * out_kernel.shape[1])
    ordered = jnp.take(latent, assign, axis=0)
    mine = lax.all_to_all(ordered, "fsdp", split_axis=0, concat_axis=2, tiled=True)
    token_rows = mine.reshape(-1, mine.shape[-1])
    embed_full, weight_full = in_one_piece((embed_weight, value_weight), "fsdp", 0, 1)
    mixed = lax.dot_general(
        token_rows, embed_full, (((1,), (1,)), ((), ())), preferred_element_type=jnp.float32
    )
    row_mean = jnp.mean(mixed, axis=-1, keepdims=True)
    centred = mixed - row_mean
    row_var = jnp.mean(centred * centred, axis=-1, keepdims=True)
    inv_std = lax.rsqrt(row_var + 1e-06)
    unit = centred * inv_std
    modulated = (unit * (1.0 + mod_scale) + mod_shift).astype(jnp.bfloat16)
    projected = jnp.dot(modulated, weight_full, preferred_element_type=jnp.float32).astype(
        jnp.bfloat16
    )
    cot_rows = value_cotangent.reshape(-1, value_cotangent.shape[-1])
    grad_mod = lax.dot_general(
        cot_rows, weight_full, (((1,), (1,)), ((), ())), preferred_element_type=jnp.float32
    )
    grad_unit = grad_mod * (1.0 + mod_scale)
    grad_mixed = inv_std * (
        grad_unit
        - jnp.mean(grad_unit, axis=-1, keepdims=True)
        - unit * jnp.mean(grad_unit * unit, axis=-1, keepdims=True)
    )
    grad_bf = grad_mixed.astype(jnp.bfloat16)
    grad_w = lax.dot_general(
        modulated, cot_rows, (((0,), (0,)), ((), ())), preferred_element_type=jnp.float32
    )
    grad_e = lax.dot_general(
        grad_bf, token_rows, (((0,), (0,)), ((), ())), preferred_element_type=jnp.float32
    )
    grad_value, grad_embed = in_one_piece_2((grad_w, grad_e), ("enc", "fsdp"), 0, 1)
    return (projected.reshape(value_cotangent.shape), grad_value, grad_embed)


def solution(mesh):
    in_specs = (
        P(None, "enc", "fsdp", None),
        P(),
        P(),
        P(),
        P(),
        P(),
        P("fsdp", None),
        P("fsdp", None),
        P("fsdp", None),
        P("fsdp", None),
        P("fsdp", "enc", None, None),
    )
    out_specs = (P("fsdp", "enc", None, None), P(("enc", "fsdp"), None), P(("enc", "fsdp"), None))
    return jax.shard_map(local, mesh=mesh, in_specs=in_specs, out_specs=out_specs, check_vma=False)
```

profile of v0, /device:TPU:1, one launch (start us, length us, event | category | flops | bytes accessed | tf_op | source)
XLA Modules:
  0.0 402.9 jit_solution(17343412539282212792)
XLA Ops:
  7.2 1.0 copy.34
  8.2 1.8 pad_maximum_fusion.1
  10.8 2.1 fusion.8
  12.9 2.3 fusion.11
  15.3 4.9 %collective-permute-start = (bf16[32,2,32,512]{3,2,1,0:T(8,128)(2,1)S(1)}, bf16[32,2,32,512]{3,2,1,0:T(8,128)(2,1)S(1)}, u32[]{:S(2)}, u32[]{:S(2)}) collective-permute-start(bf16[32,2,32,512]{3,2,1,0:T(8,128)(2,1)S(1)} %fusion.11), channel_id=1, source_target_pairs={{0,32},{32,64},{64,96},{1,33},{33,65},{65,97},{2,34},{34,66},{66,9... | collective-permute-start | bytes 6291464 | tf_op jit(solution)/shard_map/ppermute | solution.py:10
  20.3 3.2 fusion.27
  23.5 21.9 %collective-permute-done = bf16[32,2,32,512]{3,2,1,0:T(8,128)(2,1)S(1)} collective-permute-done((bf16[32,2,32,512]{3,2,1,0:T(8,128)(2,1)S(1)}, bf16[32,2,32,512]{3,2,1,0:T(8,128)(2,1)S(1)}, u32[]{:S(2)}, u32[]{:S(2)}) %collective-permute-start) | collective-permute-done | bytes 2097184 | tf_op jit(solution)/shard_map/ppermute | solution.py:10
  45.5 1.4 copy-done.3
  46.8 3.2 fusion.13
  50.0 8.0 %fusion.24 = bf16[32,2,32,16]{2,3,1,0:T(8,128)(2,1)S(1)} fusion(bf16[32,2,32,512]{3,2,1,0:T(8,128)(2,1)} %param.11, f32[32,2,32,512]{3,2,1,0:T(8,128)} %fusion.27, f32[32,2,32,512]{3,2,1,0:T(8,128)} %fusion.13, bf16[32,2,32,512]{3,2,1,0:T(8,128)(2,1)} %copy-done.3, bf16[1,3,512,512]{3,2,1,0:T(8,128)(2,1)S(1)} %copy-done.4, ...), kind=kOutput, calls=%fused_computation.32 | convolution fusion | flops 1116798976 | bytes 13205504 | tf_op jit(solution)/shard_map/dot_general | solution.py:63
  59.4 0.8 reshape.121
  60.1 10.1 %all-to-all-start = ((bf16[32,2,512]{2,1,0:T(2,128)(2,1)}), bf16[32,2,512]{2,1,0:T(2,128)(2,1)S(1)}, u32[]{:S(2)}, u32[]{:S(2)}) async-start(bf16[32,2,512]{2,1,0:T(2,128)(2,1)} %reshape.121), calls=%async_computation | async-start | bytes 131072 | tf_op jit(solution)/shard_map/all_to_all | solution.py:68
  70.5 8.5 %all-to-all-done = bf16[32,2,512]{2,1,0:T(2,128)(2,1)S(1)} async-done(((bf16[32,2,512]{2,1,0:T(2,128)(2,1)}), bf16[32,2,512]{2,1,0:T(2,128)(2,1)S(1)}, u32[]{:S(2)}, u32[]{:S(2)}) %all-to-all-start) | async-done | bytes 65568 | tf_op jit(solution)/shard_map/all_to_all | solution.py:68
  79.1 51.1 %all-gather.2.cloned.1.call-done = bf16[3072,1600]{1,0:T(8,128)(2,1)} async-done(((bf16[96,1600]{1,0:T(8,128)(2,1)}), bf16[3072,1600]{1,0:T(8,128)(2,1)}) %all-gather.2.cloned.1.call-update) | async-done | bytes 9830416 | tf_op jit(solution)/shard_map/all_gather | solution.py:16
  130.2 2.2 fusion.40
  133.2 10.0 %fusion.7 = (f32[512]{0:T(512)S(1)}, f32[3072,512]{0,1:T(8,128)S(1)}) fusion(f32[512,3072]{1,0:T(8,128)S(1)} %get-tuple-element.16, f32[3072]{0:T(1024)S(1)} %bitcast.63, f32[512]{0:T(512)S(1)} %add_rsqrt_fusion.1, f32[512]{0:T(512)S(1)} %broadcast_multiply_fusion.2, bf16[512,1536]{1,0:T(8,128)(2,1)S(1)} %bitcast.58, ...), kind=kOutput, calls=%fused_computation.11 | convolution fusion | flops 4839702016 | bytes 23611392 | tf_op jit(solution)/shard_map/dot_general | solution.py:84
  143.9 9.9 %fusion.39 = f32[3072,1536]{0,1:T(8,128)} fusion(bf16[512,1536]{1,0:T(8,128)(2,1)S(1)} %bitcast.57, f32[512,3072]{1,0:T(8,128)S(1)} %get-tuple-element.16, f32[3072]{0:T(1024)S(1)} %bitcast.69, f32[3072]{0:T(1024)S(1)} %bitcast.65, f32[512]{0:T(512)S(1)} %add_rsqrt_fusion.1, f32[512]{0:T(512)S(1)} %broadcast_multiply_fusion.2), kind=kOutput, calls=%fused_computation.59 | convolution fusion | flops 4839702528 | bytes 26767360 | tf_op jit(solution)/shard_map/dot_general | solution.py:94
  153.8 2.0 fusion.17
  155.8 16.0 %pad_maximum_fusion = f32[3072,1600]{0,1:T(8,128)} fusion(f32[3072,64]{0,1:T(8,128)S(1)} %fusion.17, f32[3072,1536]{0,1:T(8,128)} %fusion.39), kind=kLoop, calls=%fused_computation.1 | loop fusion | flops 4915200 | bytes 39321600 | tf_op jit(solution)/shard_map/concatenate | solution.py:21
  171.9 12.4 %fusion.19 = bf16[512,1536]{1,0:T(8,128)(2,1)} fusion(bf16[3072,1600]{1,0:T(8,128)(2,1)} %all-gather.2.cloned.1.call-done, f32[512,3072]{1,0:T(8,128)} %copy-done.2, f32[3072]{0:T(1024)S(1)} %bitcast.70, f32[3072]{0:T(1024)S(1)} %bitcast.67, f32[512]{0:T(512)S(1)} %add_rsqrt_fusion.1, f32[512]{0:T(512)S(1)} %broadcast_multiply_fusion.2), kind=kOutput, calls=%fused_computation.29 | convolution fusion | flops 4840488960 | bytes 17330176 | tf_op jit(solution)/shard_map/dot_general | solution.py:80
  184.3 207.6 %all-reduce.3.cloned.1.call-done = f32[3072,1600]{0,1:T(8,128)} async-done(((f32[3072,1600]{0,1:T(8,128)}), f32[3072,1600]{0,1:T(8,128)}) %all-reduce.3.cloned.1.call-update) | async-done | bytes 19660816
  391.9 1.7 constant_dynamic-slice_fusion
  393.5 0.9 copy.36
  394.4 0.9 dynamic-slice.2
  (40 shorter events, 4.7 us)
Async XLA Ops:
  7.2 126.0 %copy-start = (bf16[1,2,256,1536]{3,2,1,0:T(8,128)(2,1)S(1)}, bf16[1,2,256,1536]{3,2,1,0:T(8,128)(2,1)}, u32[]{:S(2)}) copy-start(bf16[1,2,256,1536]{3,2,1,0:T(8,128)(2,1)} %param.21) | copy-start | bytes 4718596
  7.2 13.0 %copy-start.8 = (s32[32]{0:T(128)S(1)}, s32[32]{0:T(128)}, u32[]{:S(2)}) copy-start(s32[32]{0:T(128)} %param.16) | copy-start | bytes 388
  7.2 13.1 %copy-start.4 = (bf16[1,3,512,512]{3,2,1,0:T(8,128)(2,1)S(1)}, bf16[1,3,512,512]{3,2,1,0:T(8,128)(2,1)}, u32[]{:S(2)}) copy-start(bf16[1,3,512,512]{3,2,1,0:T(8,128)(2,1)} %param.13) | copy-start | bytes 4718596
  7.2 123.0 %all-gather.2.cloned.1.call-start = ((), (), s32[]{:S(2)}) async-start(), calls=%async_computation.1 | async-start | bytes 10543104 | tf_op jit(solution)/shard_map/all_gather | solution.py:16
  15.3 30.2 %collective-permute-start = (bf16[32,2,32,512]{3,2,1,0:T(8,128)(2,1)S(1)}, bf16[32,2,32,512]{3,2,1,0:T(8,128)(2,1)S(1)}, u32[]{:S(2)}, u32[]{:S(2)}) collective-permute-start(bf16[32,2,32,512]{3,2,1,0:T(8,128)(2,1)S(1)} %fusion.11), channel_id=1, source_target_pairs={{0,32},{32,64},{64,96},{1,33},{33,65},{65,97},{2,34},{34,66},{66,9... | collective-permute-start | bytes 6291464 | tf_op jit(solution)/shard_map/ppermute | solution.py:10
  20.3 29.8 %copy-start.6 = (bf16[512,16]{0,1:T(8,128)(2,1)S(1)}, bf16[512,16]{0,1:T(8,128)(2,1)}, u32[]{:S(2)}) copy-start(bf16[512,16]{0,1:T(8,128)(2,1)} %param.14) | copy-start | bytes 49156
  45.5 1.4 copy-start.3
  50.0 20.4 %copy-start.5 = (f32[1,3072]{1,0:T(1,128)S(1)}, f32[1,3072]{1,0:T(1,128)}, u32[]{:S(2)}) copy-start(f32[1,3072]{1,0:T(1,128)} %param.19) | copy-start | bytes 36868
  60.1 18.8 %all-to-all-start = ((bf16[32,2,512]{2,1,0:T(2,128)(2,1)}), bf16[32,2,512]{2,1,0:T(2,128)(2,1)S(1)}, u32[]{:S(2)}, u32[]{:S(2)}) async-start(bf16[32,2,512]{2,1,0:T(2,128)(2,1)} %reshape.121), calls=%async_computation | async-start | bytes 131072 | tf_op jit(solution)/shard_map/all_to_all | solution.py:68
  70.2 321.7 %all-reduce.3.cloned.1.call-start = ((), (), s32[]{:S(2)}) async-start(), calls=%async_computation.2 | async-start | bytes 39321600
  132.4 21.4 %copy-start.2 = (f32[512,3072]{1,0:T(8,128)}, f32[512,3072]{1,0:T(8,128)S(1)}, u32[]{:S(2)}) copy-start(f32[512,3072]{1,0:T(8,128)S(1)} %get-tuple-element.16) | copy-start | bytes 18874372
  143.2 0.7 copy-start.7
  171.9 224.1 %copy-start.1 = (bf16[1,2,256,1536]{3,2,1,0:T(8,128)(2,1)S(1)}, bf16[1,2,256,1536]{3,2,1,0:T(8,128)(2,1)}, u32[]{:S(2)}) copy-start(bf16[1,2,256,1536]{3,2,1,0:T(8,128)(2,1)} %param.21) | copy-start | bytes 4718596
Sparse Core Ops, SparseCore 0:
  11.6 118.5 all-gather.1
  172.0 219.7 all-reduce.2
where the time goes:
time: 403 us
  waiting for transfers between devices  289 us (72%)
  matrix products  50.9 us (13%)
  other arithmetic  24.5 us (6%)
  starting transfers between devices  15.2 us (4%)
  between operations  14.3 us (4%)
  local copies, waits for them, and re-layouts  8.82 us (2%)
    unnamed x3, waiting for transfers between devices  208 us
    all_gather x1, waiting for transfers between devices, in_one_piece(): out = lax.all_gather(both, axis, axis=dim, tiled=True)  51.1 us
    ppermute x1, waiting for transfers between devices, from_behind(): return lax.ppermute(x, axis, pairs)  21.9 us
    concatenate x1, other arithmetic, in_one_piece_2(): both = jnp.concatenate(arrays, axis=along)  16 us
    dot_general x1, matrix products, local(): jnp.dot(modulated, weight_full, preferred_element_type=jnp.float32)  12.4 us
    all_to_all x1, starting transfers between devices, local(): lax.all_to_all(ordered, 'fsdp', split_axis=0, concat_axis=2, tiled=True)  10.1 us
    dot_general x1, matrix products, local(): lax.dot_general(cot_rows, weight_full, (((1,), (1,)), ((), ())), preferre...  9.99 us
    dot_general x1, matrix products, local(): lax.dot_general(modulated, cot_rows, (((0,), (0,)), ((), ())), preferred_...  9.89 us
  transfers between devices with their start and end apart: 4, of which 4 were waited for; matrix products, arithmetic and copies ran while one was open for 9% of the time, Pallas kernels for 0%

commit v1 on v0

v1 whole, which is shorter than its diff:
```python
import jax
import jax.numpy as jnp
from jax import lax
from jax.experimental import pallas as pl
from jax.experimental.pallas import tpu as pltpu
from jax.sharding import Mesh
from jax.sharding import PartitionSpec as P


BF = jnp.bfloat16
F32 = jnp.float32
AXES = ("zl", "c", "zh", "x", "y")
SIZES = (2, 2, 2, 4, 4)


def hop(values, dest):
    pairs = []
    for i in range(128):
        at, rest = {}, i
        for name, size in zip(reversed(AXES), reversed(SIZES)):
            at[name], rest = rest % size, rest // size
        to = {**at, **dest(at)}
        j = 0
        for name, size in zip(AXES, SIZES):
            j = j * size + to[name]
        pairs.append((i, j))
    return lax.ppermute(values, AXES, pairs)


def along(axis, by):
    def dest(at):
        if axis == "z":
            z = (at["zh"] * 2 + at["zl"] + by) % 4
            return {"zh": z // 2, "zl": z % 2}
        return {axis: (at[axis] + by) % 4}

    return dest


def by_core(first, second):
    return lambda at: (first if at["c"] == 0 else second)(at)


def swap(x, axis):
    return lax.ppermute(x, axis, [(0, 1), (1, 0)])


def pick(x, index, dim):
    return lax.dynamic_index_in_dim(x, index, dim, keepdims=False)


def place_kernel(idx, own, up, down, far, own2, up2, down2, far2, out, sems):
    c, a_at, b_at = idx[0], idx[1], idx[2]
    zh = idx[3]
    copies = []

    def put(pieces, a_first, b):
        for i in range(2):
            for j in range(2):
                a = a_first + i - 2 * i * (a_first % 2)
                z = zh + j - 2 * j * zh
                at_x = jnp.where(c == 0, a, b)
                at_y = jnp.where(c == 0, b, a)
                copies.append(
                    pltpu.make_async_copy(
                        pieces.at[i, j], out.at[z, at_x, at_y], sems.at[len(copies)]
                    )
                )

    for first, group in ((a_at, (own, up, down, far)), (3 - a_at, (own2, up2, down2, far2))):
        for pieces, back in zip(group, (0, 3, 1, 2)):
            put(pieces, first, (b_at + back) % 4)
    for copy in copies:
        copy.start()
    for copy in copies:
        copy.wait()


def nearest(at):
    z = 3 - (at["zh"] * 2 + at["zl"])
    return {"zh": z // 2, "zl": z % 2}


def place(idx, pieces, lanes):
    rows = pieces[0].shape[2]
    out = pl.pallas_call(
        place_kernel,
        out_shape=jax.ShapeDtypeStruct((2, 4, 4, rows, lanes), BF),
        in_specs=[pl.BlockSpec(memory_space=pltpu.SMEM)]
        + [pl.BlockSpec(memory_space=pltpu.HBM)] * 8,
        out_specs=pl.BlockSpec(memory_space=pltpu.VMEM),
        scratch_shapes=[pltpu.SemaphoreType.DMA((32,))],
        compiler_params=pltpu.CompilerParams(vmem_limit_bytes=24 << 20),
        cost_estimate=pl.CostEstimate(
            flops=0, transcendentals=0, bytes_accessed=128 * rows * lanes
        ),
        name="place",
    )(idx, *pieces)
    return out.reshape(32 * rows, lanes)


def conv_kernel(feat, before, normed, kernels, out_kernel, out):
    b, n = before[...], normed[...]
    channels = n.shape[-1]
    middle = jnp.concatenate([b[:, 1:], n[:, :1]], axis=1)
    total = None
    for k, window in enumerate((b, middle, n)):
        part = jnp.dot(
            window.reshape(-1, channels), kernels[k], preferred_element_type=F32
        )
        total = part if total is None else total + part
    activation = feat[...].astype(F32).reshape(total.shape)
    stored = (activation + total / (1.0 + jnp.exp(-total))).astype(BF)
    latent = jnp.dot(stored, out_kernel[...], preferred_element_type=F32)
    out[...] = latent.astype(BF).reshape(out.shape)


def conv_clips(features, first, before, normed, kernels, out_kernel):
    clips, frames, pixels, channels = normed.shape
    step, lat = 8, out_kernel.shape[1]
    block = pl.BlockSpec((step, frames, pixels, channels), lambda i: (i, 0, 0, 0))
    return pl.pallas_call(
        conv_kernel,
        grid=(clips // step,),
        out_shape=jax.ShapeDtypeStruct((clips, frames, pixels, lat), BF),
        in_specs=[
            pl.BlockSpec(
                (step, frames, pixels, channels), lambda i: (i + first // step, 0, 0, 0)
            ),
            block,
            block,
            pl.BlockSpec(kernels.shape, lambda i: (0, 0, 0)),
            pl.BlockSpec(out_kernel.shape, lambda i: (0, 0)),
        ],
        out_specs=pl.BlockSpec((step, frames, pixels, lat), lambda i: (i, 0, 0, 0)),
        compiler_params=pltpu.CompilerParams(
            dimension_semantics=("arbitrary",), vmem_limit_bytes=32 << 20
        ),
        cost_estimate=pl.CostEstimate(
            flops=clips * frames * pixels * channels * channels * 6,
            transcendentals=0,
            bytes_accessed=4 << 20,
        ),
        name="conv",
    )(features, before, normed, kernels, out_kernel)


def unit_of(tok, embed):
    mixed = lax.dot_general(
        tok, embed, (((1,), (1,)), ((), ())), preferred_element_type=F32
    )
    centred = mixed - jnp.mean(mixed, axis=-1, keepdims=True)
    inv_std = lax.rsqrt(jnp.mean(centred * centred, axis=-1, keepdims=True) + 1e-06)
    return centred * inv_std, inv_std


def forward_kernel(idx, tok, embed, scale, shift, out_all, out_kept, out_given):
    c = idx[0]
    unit, _ = unit_of(tok[...], embed[...])
    out_all[...] = (unit * (1.0 + scale[...]) + shift[...]).astype(BF)
    quarter = out_all.shape[1] // 4
    for zl in range(2):
        here = pl.ds(zl * quarter, quarter)
        at = pl.multiple_of((2 * zl + c) * quarter, 128)
        out_kept[:, here] = out_all[:, pl.ds(at, quarter)]
        at = pl.multiple_of((2 * zl + 1 - c) * quarter, 128)
        out_given[:, here] = out_all[:, pl.ds(at, quarter)]


def backward_kernel(
    idx, tok_t, tok, embed, scaling, cot_t, w_kept, w_got, out_e, grad_ref, mixed_ref, grad_bf, acc
):
    c, step = idx[0], pl.program_id(0)
    block, half = w_kept.shape
    width, lanes = grad_ref.shape
    group = 32

    def against(at, weight):
        at = pl.multiple_of(at * half, 128)
        return jnp.dot(weight[...], cot_t[pl.ds(at, half), :], preferred_element_type=F32)

    rows = pl.ds(pl.multiple_of(step * block, block), block)
    factor = jnp.concatenate([scaling[...]] * (lanes // scaling.shape[1]), axis=1)
    grad_ref[rows, :] = (against(c, w_kept) + against(1 - c, w_got)) * factor
    mixed_ref[rows, :] = jnp.dot(
        embed[...], tok_t[...], preferred_element_type=F32
    )

    @pl.when(step == 0)
    def _():
        acc[...] = jnp.zeros(acc.shape, F32)

    origin = mixed_ref[0:1, :]

    def load(first, i):
        here = pl.ds(pl.multiple_of(first + i * group, group), group)
        return here, mixed_ref[here, :] - origin, grad_ref[here, :]

    def fold(v):
        return jnp.sum(v.reshape(group // 8, 8, lanes), axis=0)

    def sums(i, carry):
        _, shifted, grad = load(step * block, i)
        for k, v in enumerate((shifted, shifted * shifted, grad, grad * shifted)):
            acc[k] += fold(v)
        return carry

    lax.fori_loop(0, block // group, sums, 0)

    @pl.when(step == pl.num_programs(0) - 1)
    def _():
        mean, square, mean_g, product = (
            jnp.sum(acc[k], axis=0, keepdims=True) * (1.0 / width) for k in range(4)
        )
        inv_std = lax.rsqrt(jnp.maximum(square - mean * mean, 0.0) + 1e-06)
        slope = (product - mean * mean_g) * inv_std * inv_std

        def finish(i, carry):
            here, shifted, grad = load(0, i)
            grad_bf[here, :] = (inv_std * (grad - mean_g - (shifted - mean) * slope)).astype(BF)
            return carry

        lax.fori_loop(0, width // group, finish, 0)
        out_e[...] = jnp.dot(grad_bf[...], tok[...], preferred_element_type=F32)


def backward_call(core, tok_t, tok, embed, scaling, cot_t, w_kept, w_got):
    width, tokens, block = embed.shape[0], tok.shape[0], 512

    def stays(a):
        return pl.BlockSpec(a.shape, lambda i, _: (0, 0))

    def by_rows(a):
        return pl.BlockSpec((block, a.shape[1]), lambda i, _: (i, 0))

    return pl.pallas_call(
        backward_kernel,
        grid_spec=pltpu.PrefetchScalarGridSpec(
            num_scalar_prefetch=1,
            grid=(width // block,),
            in_specs=[
                stays(tok_t),
                stays(tok),
                by_rows(embed),
                by_rows(scaling),
                stays(cot_t),
                by_rows(w_kept),
                by_rows(w_got),
            ],
            out_specs=pl.BlockSpec((width, tok.shape[1]), lambda i, _: (0, 0)),
            scratch_shapes=[
                pltpu.VMEM((width, tokens), F32),
                pltpu.VMEM((width, tokens), F32),
                pltpu.VMEM((width, tokens), BF),
                pltpu.VMEM((4, 8, tokens), F32),
            ],
        ),
        out_shape=jax.ShapeDtypeStruct((width, tok.shape[1]), F32),
        compiler_params=pltpu.CompilerParams(
            dimension_semantics=("arbitrary",), vmem_limit_bytes=40 << 20
        ),
        cost_estimate=pl.CostEstimate(
            flops=2 * tokens * width * cot_t.shape[0],
            transcendentals=0,
            bytes_accessed=16 << 20,
        ),
        name="backward",
    )(core, tok_t, tok, embed, scaling, cot_t, w_kept, w_got)


def values_kernel(idx, mod, weight, *rest):
    rest[-1][...] = jnp.dot(mod[...], weight[...], preferred_element_type=F32).astype(BF)


def values_call(side, mod, weight, before=None):
    tokens, width = mod.shape
    half, step = weight.shape[1], 256
    steps = half // step
    rest = [] if before is None else [before]
    return pl.pallas_call(
        values_kernel,
        grid_spec=pltpu.PrefetchScalarGridSpec(
            num_scalar_prefetch=1,
            grid=(steps,),
            in_specs=[
                pl.BlockSpec((tokens, width), lambda i, _: (0, 0)),
                pl.BlockSpec((width, step), lambda i, _: (0, i)),
            ]
            + [pl.BlockSpec(memory_space=pl.ANY)] * len(rest),
            out_specs=pl.BlockSpec((tokens, step), lambda i, idx: (0, idx[0] * steps + i)),
        ),
        out_shape=jax.ShapeDtypeStruct((tokens, 2 * half), BF),
        input_output_aliases={} if before is None else {3: 0},
        compiler_params=pltpu.CompilerParams(
            dimension_semantics=("arbitrary",), vmem_limit_bytes=32 << 20
        ),
        cost_estimate=pl.CostEstimate(
            flops=2 * tokens * width * half, transcendentals=0, bytes_accessed=7 << 20
        ),
        name="values",
    )(side, mod, weight, *rest)


def rows_call(kernel, idx, blocked, whole, outs, flops=0):
    tokens, step = blocked[0].shape[0], 256

    def by_rows(a):
        return pl.BlockSpec((step, a.shape[1]), lambda i, _: (i, 0))

    def stays(a):
        return pl.BlockSpec(a.shape, lambda i, _: (0, 0))

    return pl.pallas_call(
        kernel,
        grid_spec=pltpu.PrefetchScalarGridSpec(
            num_scalar_prefetch=1,
            grid=(tokens // step,),
            in_specs=[stays(a) if a_whole else by_rows(a) for a, a_whole in zip(blocked, whole)],
            out_specs=[by_rows(o) if o.shape[0] == tokens else stays(o) for o in outs],
        ),
        out_shape=outs,
        compiler_params=pltpu.CompilerParams(
            dimension_semantics=("arbitrary",), vmem_limit_bytes=48 << 20
        ),
        cost_estimate=pl.CostEstimate(flops=flops, transcendentals=0, bytes_accessed=16 << 20),
    )(idx, *blocked)


def exchange(latent, embed_weight, assign):
    clips, rows = latent.shape[0], embed_weight.shape[0]
    ordered = jnp.take(latent, assign, axis=0).reshape(clips, -1, 128)
    packed = jnp.concatenate([embed_weight[: rows // 2], embed_weight[rows // 2 :]], axis=1)
    packed = jnp.broadcast_to(packed, (clips,) + packed.shape)
    both = jnp.concatenate([packed, ordered], axis=1)
    both = lax.all_to_all(both, ("zh", "x", "y"), split_axis=0, concat_axis=0, tiled=True)
    embed = both[:, : rows // 2]
    embed = jnp.concatenate([embed[..., :64], embed[..., 64:]], axis=1).reshape(-1, 64)
    frames = latent.shape[1]
    tokens = both[:, rows // 2 :].reshape(clips, frames, -1, 64)
    return jnp.swapaxes(tokens, 0, 1).reshape(-1, 64), embed


def ring_reduce(part, cut, forward, back, beside=None):
    def halves(p):
        return p[:cut], p[cut:]

    far_a, far_b = halves(part(2))
    up_a, up_b = halves(part(1))
    down_a, down_b = halves(part(3))
    own_a, own_b = halves(part(0))
    send_f = jnp.concatenate([far_a, up_b], axis=0)
    send_b = jnp.concatenate([far_b, down_a], axis=0)
    got_f = hop(send_f, forward)
    got_b = hop(send_b, back)
    from_a, near_b = halves(got_f)
    from_b, near_a = halves(got_b)
    tied = lax.optimization_barrier
    one = None
    if beside is not None:
        one = beside((send_f, send_b))
        from_a, from_b, one = tied((from_a, from_b, one))
    sum_a = (up_a.astype(F32) + from_a.astype(F32)).astype(BF)
    sum_b = (down_b.astype(F32) + from_b.astype(F32)).astype(BF)
    last_a = hop(sum_a, forward)
    last_b = hop(sum_b, back)
    a = own_a.astype(F32) + near_a.astype(F32) + last_a.astype(F32)
    b = own_b.astype(F32) + near_b.astype(F32) + last_b.astype(F32)
    return jnp.concatenate([a, b], axis=0), one


def direct_reduce(part, dest):
    total = part(0).astype(F32)
    for d in (1, 3, 2):
        got = hop(part(d), dest(d))
        total = total + got.astype(F32)
    return total


def channel_norm(activation, gain_row):
    scaling = lax.rsqrt(jnp.mean(activation * activation, axis=-1, keepdims=True) + 1e-06)
    return activation * scaling * gain_row


def norm_clips(enc_features, enc_gain, clip_start):
    frame_count = enc_features.shape[1]
    enc_index = lax.axis_index("zl") * 2 + lax.axis_index("c")
    frame_ids = enc_index * frame_count + jnp.arange(frame_count, dtype=jnp.int32)
    live_mask = (frame_ids[None, :] >= clip_start[:, None]).astype(F32)[:, :, None, None]
    normed = live_mask * channel_norm(enc_features.astype(F32), enc_gain[0])
    return normed.astype(BF), live_mask


def as_patches(latent, live_mask):
    clips, frames, pixels, lat = latent.shape
    latent = latent * live_mask.astype(BF)
    return latent.reshape(clips, frames, pixels // 4, 4 * lat)


def local(
    enc_features,
    enc_gain,
    enc_kernel,
    out_kernel,
    clip_start,
    assign,
    embed_weight,
    mod_shift,
    mod_scale,
    value_weight,
    value_cotangent,
):
    pos = {name: lax.axis_index(name) for name in AXES}
    c = pos["c"]
    cols = value_cotangent.shape[-1]
    half = cols // 2
    cot_rows = value_cotangent.reshape(-1, cols)
    tokens = cot_rows.shape[0]
    tied = lax.optimization_barrier
    zh, x, y = pos["zh"], pos["x"], pos["y"]
    rows = value_weight.shape[0]
    own = lax.dynamic_slice_in_dim(value_weight, c * half, half, axis=1)
    a_at = jnp.where(c == 0, x, y)
    b_at = jnp.where(c == 0, y, x)
    got_z = hop(own, nearest)
    clips = enc_features.shape[0]

    def group(k, features):
        part = slice(k * clips // 2, (k + 1) * clips // 2)
        normed, live_mask = norm_clips(features[part], enc_gain, clip_start[part])
        before = lax.ppermute(normed, ("zl", "c"), [(0, 1), (1, 2), (2, 3)])
        return normed, before, live_mask

    def latents(k, normed, before, live_mask):
        latent = conv_clips(
            enc_features, k * clips // 2, before, normed, enc_kernel[0], out_kernel
        )
        return as_patches(latent, live_mask)

    group_a = group(0, enc_features)
    got_z, _ = tied((got_z, group_a[0]))
    pair = jnp.stack([own, got_z])
    one = hop(pair, by_core(lambda at: {"x": at["x"] ^ 1}, lambda at: {"y": at["y"] ^ 1}))
    features, _ = tied((enc_features, got_z))
    group_b = group(1, features)
    one, _ = tied((one, group_b[0]))
    other_cot = swap(cot_rows, "c")
    two = jnp.stack([pair, one])
    four = hop(two, by_core(lambda at: {"x": 3 - at["x"]}, lambda at: {"y": 3 - at["y"]}))
    ahead = by_core(along("y", 1), along("x", 1))
    behind = by_core(along("y", 3), along("x", 3))
    up = hop(two, ahead)
    down = hop(two, behind)

    latent_a = latents(0, *group_a)
    up2 = hop(four, ahead)
    down2 = hop(four, behind)
    far = hop(up, ahead)
    latent_b = latents(1, *group_b)
    token_rows, embed_full = exchange(jnp.concatenate([latent_a, latent_b]), embed_weight, assign)
    late_cot, late_scale, _ = tied((cot_rows, mod_scale, latent_b))
    cot_t = late_cot.T
    scaling = jnp.broadcast_to((1.0 + late_scale).reshape(-1, 1), (mod_scale.shape[1], 128))
    far2 = hop(down2, behind)
    idx = jnp.stack([c, a_at, b_at, zh]).astype(jnp.int32)
    pieces = (two, up, down, far, four, up2, down2, far2)
    width = embed_full.shape[0]
    quarter = width // 4
    core = jnp.reshape(c, (1,)).astype(jnp.int32)

    modulated, kept, given = rows_call(
        forward_kernel,
        core,
        (token_rows, embed_full, mod_scale, mod_shift),
        (False, True, True, True),
        [
            jax.ShapeDtypeStruct((tokens, width), BF),
            jax.ShapeDtypeStruct((tokens, width // 2), BF),
            jax.ShapeDtypeStruct((tokens, width // 2), BF),
        ],
        flops=2 * tokens * width * 512,
    )
    got = swap(given, "c")
    weight_kept = place(idx, pieces, half)
    weight_got = swap(weight_kept, "c")
    mod_rows = jnp.concatenate([kept, got], axis=0)
    cot_both = jnp.concatenate([cot_rows, other_cot], axis=0)
    grad_w = lax.dot_general(
        mod_rows, cot_both, (((0,), (0,)), ((), ())), preferred_element_type=F32
    ).astype(BF)
    blocks_w = grad_w.reshape(4, 4, 96, cols)

    def x_at(d):
        return (pos["x"] + d) % 4

    def z_at(d):
        z = (pos["zh"] * 2 + pos["zl"] + d) % 4
        return (z % 2) * 2 + z // 2

    def cut(blocks, d):
        return jnp.where(c == 0, pick(blocks, x_at(d), 1), pick(blocks, z_at(d), 0))

    projected = values_call(core, modulated, weight_kept)

    def embed_gradient(after):
        tok, _ = tied((token_rows, after))
        grad_e = backward_call(
            core, tok.T, tok, embed_full, scaling, cot_t, weight_kept, weight_got
        )
        grad_e = grad_e.reshape(2, 2, quarter, -1)
        given = swap(pick(grad_e, 1 - c, 1).astype(BF), "c")
        return grad_e, given

    projected = values_call(1 - core, modulated, weight_got, projected)

    forward = [by_core(along("x", 1), along("z", 1)), by_core(along("z", 1), along("x", 1))]
    back = [by_core(along("x", 3), along("z", 3)), by_core(along("z", 3), along("x", 3))]
    chunk, (grad_e, given_e) = ring_reduce(
        lambda d: cut(blocks_w, d), 2, forward[0], back[0], embed_gradient
    )
    grad_e = (pick(grad_e, c, 1) + given_e.astype(F32)).astype(BF).reshape(4, 4, 96, -1)
    chunk_e = direct_reduce(
        lambda d: cut(grad_e, d), lambda d: by_core(along("x", d), along("z", d))
    )
    chunk = jnp.concatenate([chunk.astype(BF), chunk_e.astype(BF)], axis=-1)

    def second(d):
        return pick(chunk, jnp.where(c == 0, z_at(d), x_at(d)), 0)

    rows, _ = ring_reduce(second, 48, forward[1], back[1])
    rows = rows.reshape(4, 24, -1)
    summed = direct_reduce(lambda d: pick(rows, (pos["y"] + d) % 4, 0), lambda d: along("y", d))
    grad_value = summed[:, :cols]
    grad_embed = summed[:, cols:]

    return (projected.reshape(value_cotangent.shape), grad_value, grad_embed)


def solution(mesh):
    sub = Mesh(mesh.devices.reshape(SIZES), AXES)
    enc, fsdp = ("zl", "c"), ("zh", "x", "y")
    in_specs = (
        P(None, enc, fsdp, None),
        P(),
        P(),
        P(),
        P(),
        P(),
        P(fsdp, None),
        P(fsdp, None),
        P(fsdp, None),
        P(fsdp, None),
        P(fsdp, enc, None, None),
    )
    out_specs = (P(fsdp, enc, None, None), P(enc + fsdp, None), P(enc + fsdp, None))
    return jax.shard_map(local, mesh=sub, in_specs=in_specs, out_specs=out_specs, check_vma=False)
```

time: 403 us -> 175 us (0.43)
  the two profiles are of different devices: /device:TPU:1 before, /device:TPU:0 now
where the time goes in v1:
time: 175 us; the launch traced here: 174 us
  starting transfers between devices  45.8 us (26%)
  Pallas kernels  42.3 us (24%)
  waiting for transfers between devices  35.9 us (21%)
  local copies, waits for them, and re-layouts  21.9 us (13%)
  other arithmetic  19.5 us (11%)
  matrix products  7.55 us (4%)
    ppermute x23, starting transfers between devices, hop(): return lax.ppermute(values, AXES, pairs)  35.2 us
    ppermute x23, waiting for transfers between devices, hop(): return lax.ppermute(values, AXES, pairs)  32.2 us
    pallas_call x1, Pallas kernels, backward_call(): pl.pallas_call(backward_kernel, grid_spec=pltpu.PrefetchScalarGridSpec(nu...  13.3 us
    pallas_call x2, Pallas kernels, values_call(): pl.pallas_call(values_kernel, grid_spec=pltpu.PrefetchScalarGridSpec(num_...  11.3 us
    unnamed x57, local copies, waits for them, and re-layouts  8.61 us
    dot_general x1, matrix products, local(): lax.dot_general(mod_rows, cot_both, (((0,), (0,)), ((), ())), preferred_e...  7.55 us
    pallas_call x2, Pallas kernels, conv_clips(): pl.pallas_call(conv_kernel, grid=(clips // step,), out_shape=jax.ShapeDty...  7.34 us
    pallas_call x1, Pallas kernels, place(): pl.pallas_call(place_kernel, out_shape=jax.ShapeDtypeStruct((2, 4, 4, row...  6.09 us
  transfers between devices with their start and end apart: 30, of which 7 were waited for; matrix products, arithmetic and copies ran while one was open for 19% of the time, Pallas kernels for 24%

profile of v1, /device:TPU:0, one launch (start us, length us, event | category | flops | bytes accessed | tf_op | source)
XLA Modules:
  0.0 174.3 jit_solution(8130340876463919973)
XLA Ops:
  2.3 4.1 %collective-permute-start.1 = (bf16[96,768]{1,0:T(8,128)(2,1)}, bf16[96,768]{1,0:T(8,128)(2,1)}, u32[]{:S(2)}, u32[]{:S(2)}) collective-permute-start(bf16[96,768]{1,0:T(8,128)(2,1)} %constant_dynamic-slice_fusion), channel_id=1, source_target_pairs={{0,80},{1,81},{2,82},{3,83},{4,84},{5,85},{6,86},{7,87},{8,88},{9,... | collective-permute-start | bytes 442376 | tf_op jit(solution)/shard_map/ppermute | solution.py:27
  10.6 2.5 %collective-permute-start = (bf16[16,2,32,512]{3,2,1,0:T(8,128)(2,1)S(1)}, bf16[16,2,32,512]{3,2,1,0:T(8,128)(2,1)}, u32[]{:S(2)}, u32[]{:S(2)}) collective-permute-start(bf16[16,2,32,512]{3,2,1,0:T(8,128)(2,1)S(1)} %fusion.9.normed), channel_id=1, source_target_pairs={{0,32},{32,64},{64,96},{1,33},{33,65},{65,97},{2,34},{34,66},{66,9... | collective-permute-start | bytes 3145736 | tf_op jit(solution)/shard_map/ppermute | solution.py:430
  18.4 2.3 %collective-permute-start.2 = (bf16[16,2,32,512]{3,2,1,0:T(8,128)(2,1)}, bf16[16,2,32,512]{3,2,1,0:T(8,128)(2,1)}, u32[]{:S(2)}, u32[]{:S(2)}) collective-permute-start(bf16[16,2,32,512]{3,2,1,0:T(8,128)(2,1)} %fusion.13.normed), channel_id=1, source_target_pairs={{0,32},{32,64},{64,96},{1,33},{33,65},{65,97},{2,34},{34,66},{66,9... | collective-permute-start | bytes 3145736 | tf_op jit(solution)/shard_map/ppermute | solution.py:430
  23.1 2.8 %collective-permute-start.7 = (bf16[2,2,96,768]{3,2,1,0:T(8,128)(2,1)}, bf16[2,2,96,768]{3,2,1,0:T(8,128)(2,1)}, u32[]{:S(2)}, u32[]{:S(2)}) collective-permute-start(bf16[2,2,96,768]{3,2,1,0:T(8,128)(2,1)} %pad_maximum_fusion.5.own), channel_id=1, source_target_pairs={{0,12},{1,13},{2,14},{3,15},{4,8},{5,9},{6,10},{7,11},{8,4},{9,5},... | collective-permute-start | bytes 1769480 | tf_op jit(solution)/shard_map/ppermute | solution.py:27
  27.6 12.8 %collective-permute-done.7.own2 = bf16[2,2,96,768]{3,2,1,0:T(8,128)(2,1)} collective-permute-done((bf16[2,2,96,768]{3,2,1,0:T(8,128)(2,1)}, bf16[2,2,96,768]{3,2,1,0:T(8,128)(2,1)}, u32[]{:S(2)}, u32[]{:S(2)}) %collective-permute-start.7) | collective-permute-done | bytes 589856 | tf_op jit(solution)/shard_map/ppermute | solution.py:27
  41.6 3.6 %conv.2 = bf16[16,2,32,16]{3,2,1,0:T(8,128)(2,1)S(1)} custom-call(bf16[32,2,32,512]{3,2,1,0:T(8,128)(2,1)S(1)} %copy-done.2, bf16[16,2,32,512]{3,2,1,0:T(8,128)(2,1)} %collective-permute-done.before, bf16[16,2,32,512]{3,2,1,0:T(8,128)(2,1)S(1)} %fusion.9.normed, bf16[3,512,512]{2,1,0:T(8,128)(2,1)S(1)} %bitcast.112, bf16[512,16]{1,0:T(8,128)(2,1)S(1)} %copy-done.6), custom_call_target="tpu_custom_call" | custom-call | flops 1610612736 | bytes 4194304 | tf_op jit(solution)/shard_map/conv/pallas_call | solution.py:122
  46.9 3.7 %conv.3 = bf16[16,2,32,16]{3,2,1,0:T(8,128)(2,1)S(1)} custom-call(bf16[32,2,32,512]{3,2,1,0:T(8,128)(2,1)S(1)} %copy-done.2, bf16[16,2,32,512]{3,2,1,0:T(8,128)(2,1)} %collective-permute-done.2.before, bf16[16,2,32,512]{3,2,1,0:T(8,128)(2,1)} %fusion.13.normed, bf16[3,512,512]{2,1,0:T(8,128)(2,1)S(1)} %bitcast.113, bf16[512,16]{1,0:T(8,128)(2,1)S(1)} %copy-done.6), custom_call_target="tpu_custom_call" | custom-call | flops 1610612736 | bytes 4194304 | tf_op jit(solution)/shard_map/conv/pallas_call | solution.py:122
  52.6 4.9 %all-to-all-start = ((bf16[32,56,128]{2,1,0:T(8,128)(2,1)}), bf16[32,56,128]{2,1,0:T(8,128)(2,1)S(1)}, u32[]{:S(2)}, u32[]{:S(2)}) async-start(bf16[32,56,128]{2,1,0:T(8,128)(2,1)} %pad_maximum_fusion.6), calls=%async_computation | async-start | bytes 917504 | tf_op jit(solution)/shard_map/all_to_all | solution.py:335
  57.6 3.1 %collective-permute-start.5 = (bf16[2,2,96,768]{3,2,1,0:T(8,128)(2,1)}, bf16[2,2,96,768]{3,2,1,0:T(8,128)(2,1)S(1)}, u32[]{:S(2)}, u32[]{:S(2)}) collective-permute-start(bf16[2,2,96,768]{3,2,1,0:T(8,128)(2,1)} %pad_maximum_fusion.5.own), channel_id=1, source_target_pairs={{0,3},{1,0},{2,1},{3,2},{4,7},{5,4},{6,5},{7,6},{8,11},{9,8},{10,9... | collective-permute-start | bytes 1769480 | tf_op jit(solution)/shard_map/ppermute | solution.py:27
  63.4 2.5 %collective-permute-start.10 = (bf16[2,2,96,768]{3,2,1,0:T(8,128)(2,1)}, bf16[2,2,96,768]{3,2,1,0:T(8,128)(2,1)}, u32[]{:S(2)}, u32[]{:S(2)}) collective-permute-start(bf16[2,2,96,768]{3,2,1,0:T(8,128)(2,1)} %collective-permute-done.9.down2), channel_id=1, source_target_pairs={{0,3},{1,0},{2,1},{3,2},{4,7},{5,4},{6,5},{7,6},{8,11},{9,8},{10,9... | collective-permute-start | bytes 1769480 | tf_op jit(solution)/shard_map/ppermute | solution.py:27
  65.9 3.7 %all-to-all-done = bf16[32,56,128]{2,1,0:T(8,128)(2,1)S(1)} async-done(((bf16[32,56,128]{2,1,0:T(8,128)(2,1)}), bf16[32,56,128]{2,1,0:T(8,128)(2,1)S(1)}, u32[]{:S(2)}, u32[]{:S(2)}) %all-to-all-start) | async-done | bytes 458784 | tf_op jit(solution)/shard_map/all_to_all | solution.py:335
  75.4 4.4 %shard_map.130 = (bf16[512,3072]{1,0:T(8,128)(2,1)}, bf16[512,1536]{1,0:T(8,128)(2,1)S(1)}, bf16[512,1536]{1,0:T(8,128)(2,1)}) custom-call(s32[1]{0:T(128)} %bitcast.idx, bf16[512,64]{1,0:T(8,128)(2,1)S(1)} %bitcast.119, bf16[3072,64]{1,0:T(8,128)(2,1)S(1)} %bitcast.117, f32[1,3072]{1,0:T(1,128)S(1)} %copy-done.11, f32[1,3072]{1,0:T(1,128)S(1)} %copy-done.12), custom_call_target="tpu_custom_call" | custom-call | flops 1610612736 | bytes 16777216 | tf_op jit(solution)/shard_map/pallas_call | solution.py:313
  81.0 6.1 %place.1 = bf16[2,4,4,96,768]{4,3,2,1,0:T(8,128)(2,1)} custom-call(s32[4]{0:T(128)S(1)} %pad_add_fusion.idx, bf16[2,2,96,768]{3,2,1,0:T(8,128)(2,1)} %pad_maximum_fusion.5.own, bf16[2,2,96,768]{3,2,1,0:T(8,128)(2,1)} %collective-permute-done.4.up, bf16[2,2,96,768]{3,2,1,0:T(8,128)(2,1)S(1)} %collective-permute-done.5.down, ...), custom_call_target="tpu_custom_call" | custom-call | bytes 9437184 | tf_op jit(solution)/shard_map/place/pallas_call | solution.py:86
  87.9 7.6 %convolution_convert_fusion = bf16[1536,1536]{1,0:T(8,128)(2,1)S(1)} fusion(bf16[512,1536]{1,0:T(8,128)(2,1)} %collective-permute-done.12, bf16[512,1536]{1,0:T(8,128)(2,1)} %copy-done.13, bf16[512,1536]{0,1:T(8,128)(2,1)} %collective-permute-done.13, bf16[512,1536]{0,1:T(8,128)(2,1)S(1)} %copy.34), kind=kOutput, calls=%fused_computation.1 | convolution fusion | flops 4846780416 | bytes 11010048 | tf_op jit(solution)/shard_map/dot_general | solution.py:487
  99.1 2.1 %collective-permute-start.15 = (bf16[4,96,1536]{2,1,0:T(8,128)(2,1)}, bf16[4,96,1536]{2,1,0:T(8,128)(2,1)}, u32[]{:S(2)}, u32[]{:S(2)}) collective-permute-start(bf16[4,96,1536]{2,1,0:T(8,128)(2,1)} %pad_maximum_fusion.2), channel_id=1, source_target_pairs={{0,4},{1,5},{2,6},{3,7},{4,8},{5,9},{6,10},{7,11},{8,12},{9,13},{1... | collective-permute-start | bytes 3538952 | tf_op jit(solution)/shard_map/ppermute | solution.py:27
  105.6 13.3 %backward.1 = f32[3072,64]{1,0:T(8,128)S(1)} custom-call(s32[1]{0:T(128)} %bitcast.idx, bf16[64,512]{1,0:T(8,128)(2,1)S(1)} %copy.33.tok_t, bf16[512,64]{1,0:T(8,128)(2,1)S(1)} %bitcast.121, bf16[3072,64]{1,0:T(8,128)(2,1)S(1)} %bitcast.118, f32[3072,128]{1,0:T(8,128)S(1)} %broadcast_in_dim.35.scaling, bf16[1536,512]{1,0:T(8,128)(2,1)S(1)} %bitcast.114, ...), custom_call_target="tpu_custom_call" | custom-call | flops 4831838208 | bytes 16777216 | tf_op jit(solution)/shard_map/backward/pallas_call | solution.py:236
  124.9 1.9 %collective-permute-start.18 = (bf16[2,96,1536]{2,1,0:T(8,128)(2,1)}, bf16[2,96,1536]{2,1,0:T(8,128)(2,1)}, u32[]{:S(2)}, u32[]{:S(2)}) collective-permute-start(bf16[2,96,1536]{2,1,0:T(8,128)(2,1)} %add_convert_fusion.1), channel_id=1, source_target_pairs={{0,12},{1,13},{2,14},{3,15},{4,0},{5,1},{6,2},{7,3},{8,4},{9,5},{1... | collective-permute-start | bytes 1769480 | tf_op jit(solution)/shard_map/ppermute | solution.py:27
  130.0 6.0 %collective-permute-done.21 = bf16[4,96,64]{2,1,0:T(8,128)(2,1)S(1)} collective-permute-done((bf16[4,96,64]{2,1,0:T(8,128)(2,1)S(1)}, bf16[4,96,64]{2,1,0:T(8,128)(2,1)S(1)}, u32[]{:S(2)}, u32[]{:S(2)}) %collective-permute-start.21) | collective-permute-done | bytes 49184 | tf_op jit(solution)/shard_map/ppermute | solution.py:27
  137.2 2.0 %add_convert_fusion.2 = (bf16[2,96,1536]{2,1,0:T(8,128)(2,1)S(1)}, bf16[2,96,1536]{2,1,0:T(8,128)(2,1)S(1)}) fusion(bf16[2,96,1536]{2,1,0:T(8,128)(2,1)} %collective-permute-done.17, bf16[4,96,1536]{2,1,0:T(8,128)(2,1)} %collective-permute-done.14, bf16[4,96,1536]{2,1,0:T(8,128)(2,1)S(1)} %copy-done.19, bf16[2,96,1536]{2,1,0:T(8,128)(2,1)} %collective-permute-done.18, ...), kind=kLoop, calls=%fused_computation.29 | loop fusion | flops 3538944 | bytes 4718592 | tf_op jit(solution)/shard_map/convert.4
  140.3 3.2 %collective-permute-start.22 = (bf16[96,1600]{1,0:T(8,128)(2,1)}, bf16[96,1600]{1,0:T(8,128)(2,1)}, u32[]{:S(2)}, u32[]{:S(2)}) collective-permute-start(bf16[96,1600]{1,0:T(8,128)(2,1)} %pad_maximum_fusion.7), channel_id=1, source_target_pairs={{0,80},{1,81},{2,82},{3,83},{4,84},{5,85},{6,86},{7,87},{8,88},{9,... | collective-permute-start | bytes 921608 | tf_op jit(solution)/shard_map/ppermute | solution.py:27
  143.5 4.2 %collective-permute-done.23 = bf16[96,1600]{1,0:T(8,128)(2,1)S(1)} collective-permute-done((bf16[96,1600]{1,0:T(8,128)(2,1)S(1)}, bf16[96,1600]{1,0:T(8,128)(2,1)S(1)}, u32[]{:S(2)}, u32[]{:S(2)}) %collective-permute-start.23) | collective-permute-done | bytes 307232 | tf_op jit(solution)/shard_map/ppermute | solution.py:27
  148.5 6.6 %collective-permute-done.24 = bf16[48,1600]{1,0:T(8,128)(2,1)} collective-permute-done((bf16[48,1600]{1,0:T(8,128)(2,1)S(1)}, bf16[48,1600]{1,0:T(8,128)(2,1)}, u32[]{:S(2)}, u32[]{:S(2)}) %collective-permute-start.24) | collective-permute-done | bytes 153632 | tf_op jit(solution)/shard_map/ppermute | solution.py:27
  156.7 5.6 %values.2.rest_0_ = bf16[512,1536]{1,0:T(8,128)(2,1)} custom-call(s32[1]{0:T(128)} %bitcast.idx, bf16[512,3072]{1,0:T(8,128)(2,1)S(1)} %copy-done.3, bf16[3072,768]{1,0:T(8,128)(2,1)} %bitcast.13.weight.w_kept), custom_call_target="tpu_custom_call" | custom-call | flops 2415919104 | bytes 7340032 | tf_op jit(solution)/shard_map/values/pallas_call | solution.py:280
  167.3 5.6 %values.3 = bf16[512,1536]{1,0:T(8,128)(2,1)} custom-call(s32[1]{0:T(128)S(6)} %sub.27.idx, bf16[512,3072]{1,0:T(8,128)(2,1)S(1)} %copy-done.3, bf16[3072,768]{1,0:T(8,128)(2,1)} %collective-permute-done.11.weight.w_got, bf16[512,1536]{1,0:T(8,128)(2,1)} %values.2.rest_0_), custom_call_target="tpu_custom_call", output_to_operand_aliasing={{}: (3, {})} | custom-call | flops 2415919104 | bytes 7340032 | tf_op jit(solution)/shard_map/values/pallas_call | solution.py:280
  (166 shorter events, 58.4 us)
Async XLA Ops:
  2.3 11.9 %collective-permute-start.1 = (bf16[96,768]{1,0:T(8,128)(2,1)}, bf16[96,768]{1,0:T(8,128)(2,1)}, u32[]{:S(2)}, u32[]{:S(2)}) collective-permute-start(bf16[96,768]{1,0:T(8,128)(2,1)} %constant_dynamic-slice_fusion), channel_id=1, source_target_pairs={{0,80},{1,81},{2,82},{3,83},{4,84},{5,85},{6,86},{7,87},{8,88},{9,... | collective-permute-start | bytes 442376 | tf_op jit(solution)/shard_map/ppermute | solution.py:27
  10.6 31.0 %collective-permute-start = (bf16[16,2,32,512]{3,2,1,0:T(8,128)(2,1)S(1)}, bf16[16,2,32,512]{3,2,1,0:T(8,128)(2,1)}, u32[]{:S(2)}, u32[]{:S(2)}) collective-permute-start(bf16[16,2,32,512]{3,2,1,0:T(8,128)(2,1)S(1)} %fusion.9.normed), channel_id=1, source_target_pairs={{0,32},{32,64},{64,96},{1,33},{33,65},{65,97},{2,34},{34,66},{66,9... | collective-permute-start | bytes 3145736 | tf_op jit(solution)/shard_map/ppermute | solution.py:430
  18.4 27.1 %collective-permute-start.2 = (bf16[16,2,32,512]{3,2,1,0:T(8,128)(2,1)}, bf16[16,2,32,512]{3,2,1,0:T(8,128)(2,1)}, u32[]{:S(2)}, u32[]{:S(2)}) collective-permute-start(bf16[16,2,32,512]{3,2,1,0:T(8,128)(2,1)} %fusion.13.normed), channel_id=1, source_target_pairs={{0,32},{32,64},{64,96},{1,33},{33,65},{65,97},{2,34},{34,66},{66,9... | collective-permute-start | bytes 3145736 | tf_op jit(solution)/shard_map/ppermute | solution.py:430
  23.1 17.3 %collective-permute-start.7 = (bf16[2,2,96,768]{3,2,1,0:T(8,128)(2,1)}, bf16[2,2,96,768]{3,2,1,0:T(8,128)(2,1)}, u32[]{:S(2)}, u32[]{:S(2)}) collective-permute-start(bf16[2,2,96,768]{3,2,1,0:T(8,128)(2,1)} %pad_maximum_fusion.5.own), channel_id=1, source_target_pairs={{0,12},{1,13},{2,14},{3,15},{4,8},{5,9},{6,10},{7,11},{8,4},{9,5},... | collective-permute-start | bytes 1769480 | tf_op jit(solution)/shard_map/ppermute | solution.py:27
  26.0 36.6 %collective-permute-start.4 = (bf16[2,2,96,768]{3,2,1,0:T(8,128)(2,1)}, bf16[2,2,96,768]{3,2,1,0:T(8,128)(2,1)}, u32[]{:S(2)}, u32[]{:S(2)}) collective-permute-start(bf16[2,2,96,768]{3,2,1,0:T(8,128)(2,1)} %pad_maximum_fusion.5.own), channel_id=1, source_target_pairs={{0,1},{1,2},{2,3},{3,0},{4,5},{5,6},{6,7},{7,4},{8,9},{9,10},{10,1... | collective-permute-start | bytes 1769480 | tf_op jit(solution)/shard_map/ppermute | solution.py:27
  40.4 23.0 %collective-permute-start.9 = (bf16[2,2,96,768]{3,2,1,0:T(8,128)(2,1)}, bf16[2,2,96,768]{3,2,1,0:T(8,128)(2,1)}, u32[]{:S(2)}, u32[]{:S(2)}) collective-permute-start(bf16[2,2,96,768]{3,2,1,0:T(8,128)(2,1)} %collective-permute-done.7.own2), channel_id=1, source_target_pairs={{0,3},{1,0},{2,1},{3,2},{4,7},{5,4},{6,5},{7,6},{8,11},{9,8},{10,9... | collective-permute-start | bytes 1769480 | tf_op jit(solution)/shard_map/ppermute | solution.py:27
  52.6 16.9 %all-to-all-start = ((bf16[32,56,128]{2,1,0:T(8,128)(2,1)}), bf16[32,56,128]{2,1,0:T(8,128)(2,1)S(1)}, u32[]{:S(2)}, u32[]{:S(2)}) async-start(bf16[32,56,128]{2,1,0:T(8,128)(2,1)} %pad_maximum_fusion.6), calls=%async_computation | async-start | bytes 917504 | tf_op jit(solution)/shard_map/all_to_all | solution.py:335
  57.6 22.1 %collective-permute-start.5 = (bf16[2,2,96,768]{3,2,1,0:T(8,128)(2,1)}, bf16[2,2,96,768]{3,2,1,0:T(8,128)(2,1)S(1)}, u32[]{:S(2)}, u32[]{:S(2)}) collective-permute-start(bf16[2,2,96,768]{3,2,1,0:T(8,128)(2,1)} %pad_maximum_fusion.5.own), channel_id=1, source_target_pairs={{0,3},{1,0},{2,1},{3,2},{4,7},{5,4},{6,5},{7,6},{8,11},{9,8},{10,9... | collective-permute-start | bytes 1769480 | tf_op jit(solution)/shard_map/ppermute | solution.py:27
  62.4 25.5 %collective-permute-start.13 = (bf16[512,1536]{0,1:T(8,128)(2,1)S(1)}, bf16[512,1536]{0,1:T(8,128)(2,1)}, u32[]{:S(2)}, u32[]{:S(2)}) collective-permute-start(bf16[512,1536]{0,1:T(8,128)(2,1)S(1)} %copy.34), channel_id=1, source_target_pairs={{0,32},{32,0},{1,33},{33,1},{2,34},{34,2},{3,35},{35,3},{4,36},{36... | collective-permute-start | bytes 4718600 | tf_op jit(solution)/shard_map/ppermute | solution.py:45
  62.5 18.5 %collective-permute-start.8 = (bf16[2,2,96,768]{3,2,1,0:T(8,128)(2,1)}, bf16[2,2,96,768]{3,2,1,0:T(8,128)(2,1)S(1)}, u32[]{:S(2)}, u32[]{:S(2)}) collective-permute-start(bf16[2,2,96,768]{3,2,1,0:T(8,128)(2,1)} %collective-permute-done.7.own2), channel_id=1, source_target_pairs={{0,1},{1,2},{2,3},{3,0},{4,5},{5,6},{6,7},{7,4},{8,9},{9,10},{10,1... | collective-permute-start | bytes 1769480 | tf_op jit(solution)/shard_map/ppermute | solution.py:27
  62.6 18.4 %collective-permute-start.6 = (bf16[2,2,96,768]{3,2,1,0:T(8,128)(2,1)}, bf16[2,2,96,768]{3,2,1,0:T(8,128)(2,1)}, u32[]{:S(2)}, u32[]{:S(2)}) collective-permute-start(bf16[2,2,96,768]{3,2,1,0:T(8,128)(2,1)} %collective-permute-done.4.up), channel_id=1, source_target_pairs={{0,1},{1,2},{2,3},{3,0},{4,5},{5,6},{6,7},{7,4},{8,9},{9,10},{10,1... | collective-permute-start | bytes 1769480 | tf_op jit(solution)/shard_map/ppermute | solution.py:27
  63.4 17.6 %collective-permute-start.10 = (bf16[2,2,96,768]{3,2,1,0:T(8,128)(2,1)}, bf16[2,2,96,768]{3,2,1,0:T(8,128)(2,1)}, u32[]{:S(2)}, u32[]{:S(2)}) collective-permute-start(bf16[2,2,96,768]{3,2,1,0:T(8,128)(2,1)} %collective-permute-done.9.down2), channel_id=1, source_target_pairs={{0,3},{1,0},{2,1},{3,2},{4,7},{5,4},{6,5},{7,6},{8,11},{9,8},{10,9... | collective-permute-start | bytes 1769480 | tf_op jit(solution)/shard_map/ppermute | solution.py:27
  87.1 16.9 %collective-permute-start.11 = (bf16[3072,768]{1,0:T(8,128)(2,1)}, bf16[3072,768]{1,0:T(8,128)(2,1)}, u32[]{:S(2)}, u32[]{:S(2)}) collective-permute-start(bf16[3072,768]{1,0:T(8,128)(2,1)} %bitcast.13.weight.w_kept), channel_id=1, source_target_pairs={{0,32},{32,0},{1,33},{33,1},{2,34},{34,2},{3,35},{35,3},{4,36},{36... | collective-permute-start | bytes 14155784 | tf_op jit(solution)/shard_map/ppermute | solution.py:45
  99.1 20.0 %collective-permute-start.15 = (bf16[4,96,1536]{2,1,0:T(8,128)(2,1)}, bf16[4,96,1536]{2,1,0:T(8,128)(2,1)}, u32[]{:S(2)}, u32[]{:S(2)}) collective-permute-start(bf16[4,96,1536]{2,1,0:T(8,128)(2,1)} %pad_maximum_fusion.2), channel_id=1, source_target_pairs={{0,4},{1,5},{2,6},{3,7},{4,8},{5,9},{6,10},{7,11},{8,12},{9,13},{1... | collective-permute-start | bytes 3538952 | tf_op jit(solution)/shard_map/ppermute | solution.py:27
  102.4 17.9 %collective-permute-start.14 = (bf16[4,96,1536]{2,1,0:T(8,128)(2,1)}, bf16[4,96,1536]{2,1,0:T(8,128)(2,1)}, u32[]{:S(2)}, u32[]{:S(2)}) collective-permute-start(bf16[4,96,1536]{2,1,0:T(8,128)(2,1)} %pad_maximum_fusion.1), channel_id=1, source_target_pairs={{0,12},{1,13},{2,14},{3,15},{4,0},{5,1},{6,2},{7,3},{8,4},{9,5},{1... | collective-permute-start | bytes 3538952 | tf_op jit(solution)/shard_map/ppermute | solution.py:27
  122.5 14.6 %collective-permute-start.17 = (bf16[2,96,1536]{2,1,0:T(8,128)(2,1)}, bf16[2,96,1536]{2,1,0:T(8,128)(2,1)}, u32[]{:S(2)}, u32[]{:S(2)}) collective-permute-start(bf16[2,96,1536]{2,1,0:T(8,128)(2,1)} %add_convert_fusion.3), channel_id=1, source_target_pairs={{0,4},{1,5},{2,6},{3,7},{4,8},{5,9},{6,10},{7,11},{8,12},{9,13},{1... | collective-permute-start | bytes 1769480 | tf_op jit(solution)/shard_map/ppermute | solution.py:27
  124.9 12.3 %collective-permute-start.18 = (bf16[2,96,1536]{2,1,0:T(8,128)(2,1)}, bf16[2,96,1536]{2,1,0:T(8,128)(2,1)}, u32[]{:S(2)}, u32[]{:S(2)}) collective-permute-start(bf16[2,96,1536]{2,1,0:T(8,128)(2,1)} %add_convert_fusion.1), channel_id=1, source_target_pairs={{0,12},{1,13},{2,14},{3,15},{4,0},{5,1},{6,2},{7,3},{8,4},{9,5},{1... | collective-permute-start | bytes 1769480 | tf_op jit(solution)/shard_map/ppermute | solution.py:27
  126.9 9.2 %collective-permute-start.21 = (bf16[4,96,64]{2,1,0:T(8,128)(2,1)S(1)}, bf16[4,96,64]{2,1,0:T(8,128)(2,1)S(1)}, u32[]{:S(2)}, u32[]{:S(2)}) collective-permute-start(bf16[4,96,64]{2,1,0:T(8,128)(2,1)S(1)} %get-tuple-element.50), channel_id=1, source_target_pairs={{0,8},{1,9},{2,10},{3,11},{4,12},{5,13},{6,14},{7,15},{8,0},{9,1},... | collective-permute-start | bytes 147464 | tf_op jit(solution)/shard_map/ppermute | solution.py:27
  128.0 9.1 %collective-permute-start.20 = (bf16[4,96,64]{2,1,0:T(8,128)(2,1)S(1)}, bf16[4,96,64]{2,1,0:T(8,128)(2,1)S(1)}, u32[]{:S(2)}, u32[]{:S(2)}) collective-permute-start(bf16[4,96,64]{2,1,0:T(8,128)(2,1)S(1)} %get-tuple-element.49), channel_id=1, source_target_pairs={{0,12},{1,13},{2,14},{3,15},{4,0},{5,1},{6,2},{7,3},{8,4},{9,5},{1... | collective-permute-start | bytes 147464 | tf_op jit(solution)/shard_map/ppermute | solution.py:27
  129.8 7.3 %collective-permute-start.19 = (bf16[4,96,64]{2,1,0:T(8,128)(2,1)S(1)}, bf16[4,96,64]{2,1,0:T(8,128)(2,1)S(1)}, u32[]{:S(2)}, u32[]{:S(2)}) collective-permute-start(bf16[4,96,64]{2,1,0:T(8,128)(2,1)S(1)} %get-tuple-element.48), channel_id=1, source_target_pairs={{0,4},{1,5},{2,6},{3,7},{4,8},{5,9},{6,10},{7,11},{8,12},{9,13},{1... | collective-permute-start | bytes 147464 | tf_op jit(solution)/shard_map/ppermute | solution.py:27
  139.5 8.3 %collective-permute-start.23 = (bf16[96,1600]{1,0:T(8,128)(2,1)S(1)}, bf16[96,1600]{1,0:T(8,128)(2,1)S(1)}, u32[]{:S(2)}, u32[]{:S(2)}) collective-permute-start(bf16[96,1600]{1,0:T(8,128)(2,1)S(1)} %pad_maximum_fusion.8), channel_id=1, source_target_pairs={{0,64},{1,65},{2,66},{3,67},{4,68},{5,69},{6,70},{7,71},{8,72},{9,... | collective-permute-start | bytes 921608 | tf_op jit(solution)/shard_map/ppermute | solution.py:27
  140.3 8.2 %collective-permute-start.22 = (bf16[96,1600]{1,0:T(8,128)(2,1)}, bf16[96,1600]{1,0:T(8,128)(2,1)}, u32[]{:S(2)}, u32[]{:S(2)}) collective-permute-start(bf16[96,1600]{1,0:T(8,128)(2,1)} %pad_maximum_fusion.7), channel_id=1, source_target_pairs={{0,80},{1,81},{2,82},{3,83},{4,84},{5,85},{6,86},{7,87},{8,88},{9,... | collective-permute-start | bytes 921608 | tf_op jit(solution)/shard_map/ppermute | solution.py:27
  163.5 9.5 %collective-permute-start.28 = (f32[24,1600]{1,0:T(8,128)S(1)}, f32[24,1600]{1,0:T(8,128)S(1)}, u32[]{:S(2)}, u32[]{:S(2)}) collective-permute-start(f32[24,1600]{1,0:T(8,128)S(1)} %get-tuple-element.44), channel_id=1, source_target_pairs={{0,2},{1,3},{2,0},{3,1},{4,6},{5,7},{6,4},{7,5},{8,10},{9,11},{10,... | collective-permute-start | bytes 460808 | tf_op jit(solution)/shard_map/ppermute | solution.py:27
  165.3 7.7 %collective-permute-start.27 = (f32[24,1600]{1,0:T(8,128)S(1)}, f32[24,1600]{1,0:T(8,128)S(1)}, u32[]{:S(2)}, u32[]{:S(2)}) collective-permute-start(f32[24,1600]{1,0:T(8,128)S(1)} %get-tuple-element.45), channel_id=1, source_target_pairs={{0,3},{1,0},{2,1},{3,2},{4,7},{5,4},{6,5},{7,6},{8,11},{9,8},{10,9... | collective-permute-start | bytes 460808 | tf_op jit(solution)/shard_map/ppermute | solution.py:27
  (33 other events, 226.1 us)

commit v2 on v1

--- a/solution.py
+++ b/solution.py
@@ -97,6 +97,24 @@
         name="place",
     )(idx, *pieces)
     return out.reshape(32 * rows, lanes)
+
+
+def flip_kernel(x, out):
+    out[...] = x[...].T
+
+
+def flip(x):
+    rows, cols = x.shape
+    step = 384
+    return pl.pallas_call(
+        flip_kernel,
+        grid=(cols // step,),
+        out_shape=jax.ShapeDtypeStruct((cols, rows), x.dtype),
+        in_specs=[pl.BlockSpec((rows, step), lambda i: (0, i))],
+        out_specs=pl.BlockSpec((step, rows), lambda i: (i, 0)),
+        cost_estimate=pl.CostEstimate(flops=0, transcendentals=0, bytes_accessed=4 * rows * cols),
+        name="flip",
+    )(x)
 
 
 def conv_kernel(feat, before, normed, kernels, out_kernel, out):
@@ -352,13 +370,13 @@
     send_b = jnp.concatenate([far_b, down_a], axis=0)
     got_f = hop(send_f, forward)
     got_b = hop(send_b, back)
-    from_a, near_b = halves(got_f)
-    from_b, near_a = halves(got_b)
     tied = lax.optimization_barrier
     one = None
     if beside is not None:
         one = beside((send_f, send_b))
-        from_a, from_b, one = tied((from_a, from_b, one))
+        got_f, got_b, one = tied((got_f, got_b, one))
+    from_a, near_b = halves(got_f)
+    from_b, near_a = halves(got_b)
     sum_a = (up_a.astype(F32) + from_a.astype(F32)).astype(BF)
     sum_b = (down_b.astype(F32) + from_b.astype(F32)).astype(BF)
     last_a = hop(sum_a, forward)
@@ -422,17 +440,18 @@
     a_at = jnp.where(c == 0, x, y)
     b_at = jnp.where(c == 0, y, x)
     got_z = hop(own, nearest)
-    clips = enc_features.shape[0]
+    bounds = (0, 16, 32)
+    kernels = pltpu.with_memory_space_constraint(enc_kernel[0], pltpu.HBM)
 
     def group(k, features):
-        part = slice(k * clips // 2, (k + 1) * clips // 2)
+        part = slice(*bounds[k : k + 2])
         normed, live_mask = norm_clips(features[part], enc_gain, clip_start[part])
         before = lax.ppermute(normed, ("zl", "c"), [(0, 1), (1, 2), (2, 3)])
         return normed, before, live_mask
 
     def latents(k, normed, before, live_mask):
         latent = conv_clips(
-            enc_features, k * clips // 2, before, normed, enc_kernel[0], out_kernel
+            enc_features, bounds[k], before, normed, kernels, out_kernel
         )
         return as_patches(latent, live_mask)
 
@@ -458,7 +477,7 @@
     latent_b = latents(1, *group_b)
     token_rows, embed_full = exchange(jnp.concatenate([latent_a, latent_b]), embed_weight, assign)
     late_cot, late_scale, _ = tied((cot_rows, mod_scale, latent_b))
-    cot_t = late_cot.T
+    cot_t = flip(late_cot)
     scaling = jnp.broadcast_to((1.0 + late_scale).reshape(-1, 1), (mod_scale.shape[1], 128))
     far2 = hop(down2, behind)
     idx = jnp.stack([c, a_at, b_at, zh]).astype(jnp.int32)
@@ -512,10 +531,10 @@
 
     projected = values_call(1 - core, modulated, weight_got, projected)
 
-    forward = [by_core(along("x", 1), along("z", 1)), by_core(along("z", 1), along("x", 1))]
-    back = [by_core(along("x", 3), along("z", 3)), by_core(along("z", 3), along("x", 3))]
+    forward = by_core(along("x", 1), along("z", 1))
+    back = by_core(along("x", 3), along("z", 3))
     chunk, (grad_e, given_e) = ring_reduce(
-        lambda d: cut(blocks_w, d), 2, forward[0], back[0], embed_gradient
+        lambda d: cut(blocks_w, d), 2, forward, back, embed_gradient
     )
     grad_e = (pick(grad_e, c, 1) + given_e.astype(F32)).astype(BF).reshape(4, 4, 96, -1)
     chunk_e = direct_reduce(
@@ -526,7 +545,7 @@
     def second(d):
         return pick(chunk, jnp.where(c == 0, z_at(d), x_at(d)), 0)
 
-    rows, _ = ring_reduce(second, 48, forward[1], back[1])
+    rows = direct_reduce(second, lambda d: by_core(along("z", d), along("x", d)))
     rows = rows.reshape(4, 24, -1)
     summed = direct_reduce(lambda d: pick(rows, (pos["y"] + d) % 4, 0), lambda d: along("y", d))
     grad_value = summed[:, :cols]

time: 175 us -> 181 us (1.034)
  the two profiles are of different devices: /device:TPU:0 before, /device:TPU:1 now
where the time goes in v2:
time: 181 us; the launch traced here: 178 us
  starting transfers between devices  53.9 us (30%)
  Pallas kernels  48.2 us (27%)
  waiting for transfers between devices  32.1 us (18%)
  other arithmetic  21.6 us (12%)
  local copies, waits for them, and re-layouts  13.6 us (8%)
  matrix products  7.32 us (4%)
    ppermute x22, starting transfers between devices, hop(): return lax.ppermute(values, AXES, pairs)  32.2 us
    ppermute x22, waiting for transfers between devices, hop(): return lax.ppermute(values, AXES, pairs)  30.4 us
    pallas_call x1, Pallas kernels, backward_call(): pl.pallas_call(backward_kernel, grid_spec=pltpu.PrefetchScalarGridSpec(nu...  13.4 us
    pallas_call x2, Pallas kernels, values_call(): pl.pallas_call(values_kernel, grid_spec=pltpu.PrefetchScalarGridSpec(num_...  11.2 us
    ppermute x4, starting transfers between devices, swap(): return lax.ppermute(x, axis, [(0, 1), (1, 0)])  11.2 us
    pallas_call x2, Pallas kernels, conv_clips(): pl.pallas_call(conv_kernel, grid=(clips // step,), out_shape=jax.ShapeDty...  8.43 us
    dot_general x1, matrix products, local(): lax.dot_general(mod_rows, cot_both, (((0,), (0,)), ((), ())), preferred_e...  7.32 us
    pallas_call x1, Pallas kernels, place(): pl.pallas_call(place_kernel, out_shape=jax.ShapeDtypeStruct((2, 4, 4, row...  6.83 us
  transfers between devices with their start and end apart: 29, of which 11 were waited for; matrix products, arithmetic and copies ran while one was open for 13% of the time, Pallas kernels for 27%

profile of v2, /device:TPU:1, one launch (start us, length us, event | category | flops | bytes accessed | tf_op | source)
XLA Modules:
  0.0 177.8 jit_solution(14457095956390209456)
XLA Ops:
  2.3 4.6 %collective-permute-start.1 = (bf16[96,768]{1,0:T(8,128)(2,1)}, bf16[96,768]{1,0:T(8,128)(2,1)}, u32[]{:S(2)}, u32[]{:S(2)}) collective-permute-start(bf16[96,768]{1,0:T(8,128)(2,1)} %constant_dynamic-slice_fusion), channel_id=1, source_target_pairs={{0,80},{1,81},{2,82},{3,83},{4,84},{5,85},{6,86},{7,87},{8,88},{9,... | collective-permute-start | bytes 442376 | tf_op jit(solution)/shard_map/ppermute | solution.py:27
  11.0 2.3 %collective-permute-start = (bf16[16,2,32,512]{3,2,1,0:T(8,128)(2,1)S(1)}, bf16[16,2,32,512]{3,2,1,0:T(8,128)(2,1)}, u32[]{:S(2)}, u32[]{:S(2)}) collective-permute-start(bf16[16,2,32,512]{3,2,1,0:T(8,128)(2,1)S(1)} %fusion.9.normed), channel_id=1, source_target_pairs={{0,32},{32,64},{64,96},{1,33},{33,65},{65,97},{2,34},{34,66},{66,9... | collective-permute-start | bytes 3145736 | tf_op jit(solution)/shard_map/ppermute | solution.py:449
  22.4 2.7 %collective-permute-start.7 = (bf16[2,2,96,768]{3,2,1,0:T(8,128)(2,1)}, bf16[2,2,96,768]{3,2,1,0:T(8,128)(2,1)}, u32[]{:S(2)}, u32[]{:S(2)}) collective-permute-start(bf16[2,2,96,768]{3,2,1,0:T(8,128)(2,1)} %pad_maximum_fusion.4.own), channel_id=1, source_target_pairs={{0,12},{1,13},{2,14},{3,15},{4,8},{5,9},{6,10},{7,11},{8,4},{9,5},... | collective-permute-start | bytes 1769480 | tf_op jit(solution)/shard_map/ppermute | solution.py:27
  26.6 7.5 %collective-permute-done.7.own2 = bf16[2,2,96,768]{3,2,1,0:T(8,128)(2,1)} collective-permute-done((bf16[2,2,96,768]{3,2,1,0:T(8,128)(2,1)}, bf16[2,2,96,768]{3,2,1,0:T(8,128)(2,1)}, u32[]{:S(2)}, u32[]{:S(2)}) %collective-permute-start.7) | collective-permute-done | bytes 589856 | tf_op jit(solution)/shard_map/ppermute | solution.py:27
  34.0 4.8 %collective-permute-start.9 = (bf16[2,2,96,768]{3,2,1,0:T(8,128)(2,1)}, bf16[2,2,96,768]{3,2,1,0:T(8,128)(2,1)}, u32[]{:S(2)}, u32[]{:S(2)}) collective-permute-start(bf16[2,2,96,768]{3,2,1,0:T(8,128)(2,1)} %collective-permute-done.7.own2), channel_id=1, source_target_pairs={{0,3},{1,0},{2,1},{3,2},{4,7},{5,4},{6,5},{7,6},{8,11},{9,8},{10,9... | collective-permute-start | bytes 1769480 | tf_op jit(solution)/shard_map/ppermute | solution.py:27
  38.8 4.1 %conv.2 = bf16[16,2,32,16]{3,2,1,0:T(8,128)(2,1)S(1)} custom-call(bf16[32,2,32,512]{3,2,1,0:T(8,128)(2,1)S(1)} %copy-done.2, bf16[16,2,32,512]{3,2,1,0:T(8,128)(2,1)} %collective-permute-done.before, bf16[16,2,32,512]{3,2,1,0:T(8,128)(2,1)S(1)} %fusion.9.normed, bf16[3,512,512]{2,1,0:T(8,128)(2,1)} %bitcast.100, bf16[512,16]{1,0:T(8,128)(2,1)S(1)} %copy-done.5), custom_call_target="tpu_custom_call" | custom-call | flops 1610612736 | bytes 4194304 | tf_op jit(solution)/shard_map/conv/pallas_call | solution.py:140
  43.2 4.3 %conv.3 = bf16[16,2,32,16]{3,2,1,0:T(8,128)(2,1)S(1)} custom-call(bf16[32,2,32,512]{3,2,1,0:T(8,128)(2,1)S(1)} %copy-done.2, bf16[16,2,32,512]{3,2,1,0:T(8,128)(2,1)} %collective-permute-done.2.before, bf16[16,2,32,512]{3,2,1,0:T(8,128)(2,1)} %fusion.13.normed, bf16[3,512,512]{2,1,0:T(8,128)(2,1)} %bitcast.101, bf16[512,16]{1,0:T(8,128)(2,1)S(1)} %copy-done.5), custom_call_target="tpu_custom_call" | custom-call | flops 1610612736 | bytes 4194304 | tf_op jit(solution)/shard_map/conv/pallas_call | solution.py:140
  49.5 6.1 %all-to-all-start = ((bf16[32,56,128]{2,1,0:T(8,128)(2,1)}), bf16[32,56,128]{2,1,0:T(8,128)(2,1)S(1)}, u32[]{:S(2)}, u32[]{:S(2)}) async-start(bf16[32,56,128]{2,1,0:T(8,128)(2,1)} %pad_maximum_fusion.5), calls=%async_computation | async-start | bytes 917504 | tf_op jit(solution)/shard_map/all_to_all | solution.py:353
  55.7 2.5 %collective-permute-start.5 = (bf16[2,2,96,768]{3,2,1,0:T(8,128)(2,1)}, bf16[2,2,96,768]{3,2,1,0:T(8,128)(2,1)S(1)}, u32[]{:S(2)}, u32[]{:S(2)}) collective-permute-start(bf16[2,2,96,768]{3,2,1,0:T(8,128)(2,1)} %pad_maximum_fusion.4.own), channel_id=1, source_target_pairs={{0,3},{1,0},{2,1},{3,2},{4,7},{5,4},{6,5},{7,6},{8,11},{9,8},{10,9... | collective-permute-start | bytes 1769480 | tf_op jit(solution)/shard_map/ppermute | solution.py:27
  58.2 3.5 %collective-permute-start.13 = (bf16[512,1536]{1,0:T(8,128)(2,1)}, bf16[512,1536]{1,0:T(8,128)(2,1)}, u32[]{:S(2)}, u32[]{:S(2)}) collective-permute-start(bf16[512,1536]{1,0:T(8,128)(2,1)} %bitcast.15.x), channel_id=1, source_target_pairs={{0,32},{32,0},{1,33},{33,1},{2,34},{34,2},{3,35},{35,3},{4,36},{36... | collective-permute-start | bytes 4718600 | tf_op jit(solution)/shard_map/ppermute | solution.py:45
  67.7 4.4 %shard_map.130 = (bf16[512,3072]{1,0:T(8,128)(2,1)}, bf16[512,1536]{1,0:T(8,128)(2,1)S(1)}, bf16[512,1536]{1,0:T(8,128)(2,1)}) custom-call(s32[1]{0:T(128)} %bitcast.idx, bf16[512,64]{1,0:T(8,128)(2,1)S(1)} %bitcast.96, bf16[3072,64]{1,0:T(8,128)(2,1)S(1)} %bitcast.94, f32[1,3072]{1,0:T(1,128)S(1)} %copy-done.8, f32[1,3072]{1,0:T(1,128)S(1)} %copy-done.9), custom_call_target="tpu_custom_call" | custom-call | flops 1610612736 | bytes 16777216 | tf_op jit(solution)/shard_map/pallas_call | solution.py:331
  73.3 4.6 %collective-permute-start.12 = (bf16[512,1536]{1,0:T(8,128)(2,1)}, bf16[512,1536]{1,0:T(8,128)(2,1)}, u32[]{:S(2)}, u32[]{:S(2)}) collective-permute-start(bf16[512,1536]{1,0:T(8,128)(2,1)} %get-tuple-element.21), channel_id=1, source_target_pairs={{0,32},{32,0},{1,33},{33,1},{2,34},{34,2},{3,35},{35,3},{4,36},{36... | collective-permute-start | bytes 4718600 | tf_op jit(solution)/shard_map/ppermute | solution.py:45
  78.5 6.8 %place.1 = bf16[2,4,4,96,768]{4,3,2,1,0:T(8,128)(2,1)} custom-call(s32[4]{0:T(128)S(1)} %pad_add_fusion.idx, bf16[2,2,96,768]{3,2,1,0:T(8,128)(2,1)} %pad_maximum_fusion.4.own, bf16[2,2,96,768]{3,2,1,0:T(8,128)(2,1)} %collective-permute-done.4.up, bf16[2,2,96,768]{3,2,1,0:T(8,128)(2,1)S(1)} %collective-permute-done.5.down, ...), custom_call_target="tpu_custom_call" | custom-call | bytes 9437184 | tf_op jit(solution)/shard_map/place/pallas_call | solution.py:86
  87.5 4.0 %flip.1.cot_t = bf16[1536,512]{1,0:T(8,128)(2,1)} custom-call(bf16[512,1536]{1,0:T(8,128)(2,1)} %bitcast.15.x), custom_call_target="tpu_custom_call" | custom-call | bytes 3145728 | tf_op jit(solution)/shard_map/flip/pallas_call | solution.py:109
  91.4 7.3 %convolution_convert_fusion = bf16[1536,1536]{1,0:T(8,128)(2,1)S(1)} fusion(bf16[512,1536]{1,0:T(8,128)(2,1)} %collective-permute-done.12, bf16[512,1536]{1,0:T(8,128)(2,1)S(1)} %copy-done.11, bf16[512,1536]{1,0:T(8,128)(2,1)} %collective-permute-done.13, bf16[512,1536]{1,0:T(8,128)(2,1)} %bitcast.15.x), kind=kOutput, calls=%fused_computation.1 | convolution fusion | flops 4846780416 | bytes 11010048 | tf_op jit(solution)/shard_map/dot_general | solution.py:506
  103.6 2.7 %collective-permute-start.15 = (bf16[4,96,1536]{2,1,0:T(8,128)(2,1)}, bf16[4,96,1536]{2,1,0:T(8,128)(2,1)}, u32[]{:S(2)}, u32[]{:S(2)}) collective-permute-start(bf16[4,96,1536]{2,1,0:T(8,128)(2,1)} %pad_maximum_fusion.2), channel_id=1, source_target_pairs={{0,12},{1,13},{2,14},{3,15},{4,0},{5,1},{6,2},{7,3},{8,4},{9,5},{1... | collective-permute-start | bytes 3538952 | tf_op jit(solution)/shard_map/ppermute | solution.py:27
  108.0 13.4 %backward.1 = f32[3072,64]{1,0:T(8,128)S(1)} custom-call(s32[1]{0:T(128)} %bitcast.idx, bf16[64,512]{1,0:T(8,128)(2,1)S(1)} %copy.30.tok_t, bf16[512,64]{1,0:T(8,128)(2,1)S(1)} %bitcast.98, bf16[3072,64]{1,0:T(8,128)(2,1)S(1)} %bitcast.95, f32[3072,128]{1,0:T(8,128)S(1)} %broadcast_in_dim.35.scaling, bf16[1536,512]{1,0:T(8,128)(2,1)S(1)} %copy-done.4, ...), custom_call_target="tpu_custom_call" | custom-call | flops 4831838208 | bytes 16777216 | tf_op jit(solution)/shard_map/backward/pallas_call | solution.py:254
  123.7 2.2 %add_convert_fusion.3 = bf16[2,96,1536]{2,1,0:T(8,128)(2,1)} fusion(bf16[4,96,1536]{2,1,0:T(8,128)(2,1)S(1)} %copy-done.14, bf16[4,96,1536]{2,1,0:T(8,128)(2,1)} %collective-permute-done.14), kind=kLoop, calls=%fused_computation.30 | loop fusion | flops 1179648 | bytes 1769472 | tf_op jit(solution)/shard_map/convert_element_type | solution.py:380
  125.9 10.6 %collective-permute-done.17 = bf16[2,96,1536]{2,1,0:T(8,128)(2,1)} collective-permute-done((bf16[2,96,1536]{2,1,0:T(8,128)(2,1)}, bf16[2,96,1536]{2,1,0:T(8,128)(2,1)}, u32[]{:S(2)}, u32[]{:S(2)}) %collective-permute-start.17) | collective-permute-done | bytes 589856 | tf_op jit(solution)/shard_map/ppermute | solution.py:27
  136.5 3.1 %add_convert_fusion.2 = (bf16[2,96,1536]{2,1,0:T(8,128)(2,1)}, bf16[2,96,1536]{2,1,0:T(8,128)(2,1)}) fusion(bf16[2,96,1536]{2,1,0:T(8,128)(2,1)} %collective-permute-done.17, bf16[4,96,1536]{2,1,0:T(8,128)(2,1)} %get-tuple-element.29, bf16[4,96,1536]{2,1,0:T(8,128)(2,1)} %collective-permute-done.15, bf16[4,96,1536]{2,1,0:T(8,128)(2,1)S(1)} %copy-done.16), kind=kLoop, calls=%fused_computation.29 | loop fusion | flops 2949120 | bytes 4128768 | tf_op jit(solution)/shard_map/convert.1
  141.3 2.3 %collective-permute-start.20 = (bf16[4,96,64]{2,1,0:T(8,128)(2,1)S(1)}, bf16[4,96,64]{2,1,0:T(8,128)(2,1)S(1)}, u32[]{:S(2)}, u32[]{:S(2)}) collective-permute-start(bf16[4,96,64]{2,1,0:T(8,128)(2,1)S(1)} %get-tuple-element.46), channel_id=1, source_target_pairs={{0,12},{1,13},{2,14},{3,15},{4,0},{5,1},{6,2},{7,3},{8,4},{9,5},{1... | collective-permute-start | bytes 147464 | tf_op jit(solution)/shard_map/ppermute | solution.py:27
  145.1 5.8 %collective-permute-done.20 = bf16[4,96,64]{2,1,0:T(8,128)(2,1)S(1)} collective-permute-done((bf16[4,96,64]{2,1,0:T(8,128)(2,1)S(1)}, bf16[4,96,64]{2,1,0:T(8,128)(2,1)S(1)}, u32[]{:S(2)}, u32[]{:S(2)}) %collective-permute-start.20) | collective-permute-done | bytes 49184 | tf_op jit(solution)/shard_map/ppermute | solution.py:27
  158.5 5.6 %values.2.rest_0_ = bf16[512,1536]{1,0:T(8,128)(2,1)} custom-call(s32[1]{0:T(128)} %bitcast.idx, bf16[512,3072]{1,0:T(8,128)(2,1)S(1)} %copy-done.3, bf16[3072,768]{1,0:T(8,128)(2,1)} %bitcast.13.weight.w_kept), custom_call_target="tpu_custom_call" | custom-call | flops 2415919104 | bytes 7340032 | tf_op jit(solution)/shard_map/values/pallas_call | solution.py:298
  170.5 5.6 %values.3 = bf16[512,1536]{1,0:T(8,128)(2,1)} custom-call(s32[1]{0:T(128)S(6)} %sub.27.idx, bf16[512,3072]{1,0:T(8,128)(2,1)S(1)} %copy-done.3, bf16[3072,768]{1,0:T(8,128)(2,1)} %collective-permute-done.11.weight.w_got, bf16[512,1536]{1,0:T(8,128)(2,1)} %values.2.rest_0_), custom_call_target="tpu_custom_call", output_to_operand_aliasing={{}: (3, {})} | custom-call | flops 2415919104 | bytes 7340032 | tf_op jit(solution)/shard_map/values/pallas_call | solution.py:298
  (154 shorter events, 56.0 us)
Async XLA Ops:
  2.3 12.1 %collective-permute-start.1 = (bf16[96,768]{1,0:T(8,128)(2,1)}, bf16[96,768]{1,0:T(8,128)(2,1)}, u32[]{:S(2)}, u32[]{:S(2)}) collective-permute-start(bf16[96,768]{1,0:T(8,128)(2,1)} %constant_dynamic-slice_fusion), channel_id=1, source_target_pairs={{0,80},{1,81},{2,82},{3,83},{4,84},{5,85},{6,86},{7,87},{8,88},{9,... | collective-permute-start | bytes 442376 | tf_op jit(solution)/shard_map/ppermute | solution.py:27
  11.0 27.7 %collective-permute-start = (bf16[16,2,32,512]{3,2,1,0:T(8,128)(2,1)S(1)}, bf16[16,2,32,512]{3,2,1,0:T(8,128)(2,1)}, u32[]{:S(2)}, u32[]{:S(2)}) collective-permute-start(bf16[16,2,32,512]{3,2,1,0:T(8,128)(2,1)S(1)} %fusion.9.normed), channel_id=1, source_target_pairs={{0,32},{32,64},{64,96},{1,33},{33,65},{65,97},{2,34},{34,66},{66,9... | collective-permute-start | bytes 3145736 | tf_op jit(solution)/shard_map/ppermute | solution.py:449
  18.4 24.8 %collective-permute-start.2 = (bf16[16,2,32,512]{3,2,1,0:T(8,128)(2,1)}, bf16[16,2,32,512]{3,2,1,0:T(8,128)(2,1)}, u32[]{:S(2)}, u32[]{:S(2)}) collective-permute-start(bf16[16,2,32,512]{3,2,1,0:T(8,128)(2,1)} %fusion.13.normed), channel_id=1, source_target_pairs={{0,32},{32,64},{64,96},{1,33},{33,65},{65,97},{2,34},{34,66},{66,9... | collective-permute-start | bytes 3145736 | tf_op jit(solution)/shard_map/ppermute | solution.py:449
  22.4 11.6 %collective-permute-start.7 = (bf16[2,2,96,768]{3,2,1,0:T(8,128)(2,1)}, bf16[2,2,96,768]{3,2,1,0:T(8,128)(2,1)}, u32[]{:S(2)}, u32[]{:S(2)}) collective-permute-start(bf16[2,2,96,768]{3,2,1,0:T(8,128)(2,1)} %pad_maximum_fusion.4.own), channel_id=1, source_target_pairs={{0,12},{1,13},{2,14},{3,15},{4,8},{5,9},{6,10},{7,11},{8,4},{9,5},... | collective-permute-start | bytes 1769480 | tf_op jit(solution)/shard_map/ppermute | solution.py:27
  25.3 37.6 %collective-permute-start.4 = (bf16[2,2,96,768]{3,2,1,0:T(8,128)(2,1)}, bf16[2,2,96,768]{3,2,1,0:T(8,128)(2,1)}, u32[]{:S(2)}, u32[]{:S(2)}) collective-permute-start(bf16[2,2,96,768]{3,2,1,0:T(8,128)(2,1)} %pad_maximum_fusion.4.own), channel_id=1, source_target_pairs={{0,1},{1,2},{2,3},{3,0},{4,5},{5,6},{6,7},{7,4},{8,9},{9,10},{10,1... | collective-permute-start | bytes 1769480 | tf_op jit(solution)/shard_map/ppermute | solution.py:27
  34.0 30.1 %collective-permute-start.9 = (bf16[2,2,96,768]{3,2,1,0:T(8,128)(2,1)}, bf16[2,2,96,768]{3,2,1,0:T(8,128)(2,1)}, u32[]{:S(2)}, u32[]{:S(2)}) collective-permute-start(bf16[2,2,96,768]{3,2,1,0:T(8,128)(2,1)} %collective-permute-done.7.own2), channel_id=1, source_target_pairs={{0,3},{1,0},{2,1},{3,2},{4,7},{5,4},{6,5},{7,6},{8,11},{9,8},{10,9... | collective-permute-start | bytes 1769480 | tf_op jit(solution)/shard_map/ppermute | solution.py:27
  49.5 16.4 %all-to-all-start = ((bf16[32,56,128]{2,1,0:T(8,128)(2,1)}), bf16[32,56,128]{2,1,0:T(8,128)(2,1)S(1)}, u32[]{:S(2)}, u32[]{:S(2)}) async-start(bf16[32,56,128]{2,1,0:T(8,128)(2,1)} %pad_maximum_fusion.5), calls=%async_computation | async-start | bytes 917504 | tf_op jit(solution)/shard_map/all_to_all | solution.py:353
  55.7 17.6 %collective-permute-start.5 = (bf16[2,2,96,768]{3,2,1,0:T(8,128)(2,1)}, bf16[2,2,96,768]{3,2,1,0:T(8,128)(2,1)S(1)}, u32[]{:S(2)}, u32[]{:S(2)}) collective-permute-start(bf16[2,2,96,768]{3,2,1,0:T(8,128)(2,1)} %pad_maximum_fusion.4.own), channel_id=1, source_target_pairs={{0,3},{1,0},{2,1},{3,2},{4,7},{5,4},{6,5},{7,6},{8,11},{9,8},{10,9... | collective-permute-start | bytes 1769480 | tf_op jit(solution)/shard_map/ppermute | solution.py:27
  58.2 33.2 %collective-permute-start.13 = (bf16[512,1536]{1,0:T(8,128)(2,1)}, bf16[512,1536]{1,0:T(8,128)(2,1)}, u32[]{:S(2)}, u32[]{:S(2)}) collective-permute-start(bf16[512,1536]{1,0:T(8,128)(2,1)} %bitcast.15.x), channel_id=1, source_target_pairs={{0,32},{32,0},{1,33},{33,1},{2,34},{34,2},{3,35},{35,3},{4,36},{36... | collective-permute-start | bytes 4718600 | tf_op jit(solution)/shard_map/ppermute | solution.py:45
  61.7 16.8 %collective-permute-start.8 = (bf16[2,2,96,768]{3,2,1,0:T(8,128)(2,1)}, bf16[2,2,96,768]{3,2,1,0:T(8,128)(2,1)S(1)}, u32[]{:S(2)}, u32[]{:S(2)}) collective-permute-start(bf16[2,2,96,768]{3,2,1,0:T(8,128)(2,1)} %collective-permute-done.7.own2), channel_id=1, source_target_pairs={{0,1},{1,2},{2,3},{3,0},{4,5},{5,6},{6,7},{7,4},{8,9},{9,10},{10,1... | collective-permute-start | bytes 1769480 | tf_op jit(solution)/shard_map/ppermute | solution.py:27
  62.9 15.6 %collective-permute-start.6 = (bf16[2,2,96,768]{3,2,1,0:T(8,128)(2,1)}, bf16[2,2,96,768]{3,2,1,0:T(8,128)(2,1)S(1)}, u32[]{:S(2)}, u32[]{:S(2)}) collective-permute-start(bf16[2,2,96,768]{3,2,1,0:T(8,128)(2,1)} %collective-permute-done.4.up), channel_id=1, source_target_pairs={{0,1},{1,2},{2,3},{3,0},{4,5},{5,6},{6,7},{7,4},{8,9},{9,10},{10,1... | collective-permute-start | bytes 1769480 | tf_op jit(solution)/shard_map/ppermute | solution.py:27
  64.1 14.4 %collective-permute-start.10 = (bf16[2,2,96,768]{3,2,1,0:T(8,128)(2,1)}, bf16[2,2,96,768]{3,2,1,0:T(8,128)(2,1)S(1)}, u32[]{:S(2)}, u32[]{:S(2)}) collective-permute-start(bf16[2,2,96,768]{3,2,1,0:T(8,128)(2,1)} %collective-permute-done.9.down2), channel_id=1, source_target_pairs={{0,3},{1,0},{2,1},{3,2},{4,7},{5,4},{6,5},{7,6},{8,11},{9,8},{10,9... | collective-permute-start | bytes 1769480 | tf_op jit(solution)/shard_map/ppermute | solution.py:27
  73.3 18.2 %collective-permute-start.12 = (bf16[512,1536]{1,0:T(8,128)(2,1)}, bf16[512,1536]{1,0:T(8,128)(2,1)}, u32[]{:S(2)}, u32[]{:S(2)}) collective-permute-start(bf16[512,1536]{1,0:T(8,128)(2,1)} %get-tuple-element.21), channel_id=1, source_target_pairs={{0,32},{32,0},{1,33},{33,1},{2,34},{34,2},{3,35},{35,3},{4,36},{36... | collective-permute-start | bytes 4718600 | tf_op jit(solution)/shard_map/ppermute | solution.py:45
  85.3 21.1 %collective-permute-start.11 = (bf16[3072,768]{1,0:T(8,128)(2,1)}, bf16[3072,768]{1,0:T(8,128)(2,1)}, u32[]{:S(2)}, u32[]{:S(2)}) collective-permute-start(bf16[3072,768]{1,0:T(8,128)(2,1)} %bitcast.13.weight.w_kept), channel_id=1, source_target_pairs={{0,32},{32,0},{1,33},{33,1},{2,34},{34,2},{3,35},{35,3},{4,36},{36... | collective-permute-start | bytes 14155784 | tf_op jit(solution)/shard_map/ppermute | solution.py:45
  102.4 20.0 %collective-permute-start.14 = (bf16[4,96,1536]{2,1,0:T(8,128)(2,1)}, bf16[4,96,1536]{2,1,0:T(8,128)(2,1)}, u32[]{:S(2)}, u32[]{:S(2)}) collective-permute-start(bf16[4,96,1536]{2,1,0:T(8,128)(2,1)} %pad_maximum_fusion.1), channel_id=1, source_target_pairs={{0,4},{1,5},{2,6},{3,7},{4,8},{5,9},{6,10},{7,11},{8,12},{9,13},{1... | collective-permute-start | bytes 3538952 | tf_op jit(solution)/shard_map/ppermute | solution.py:27
  103.6 18.8 %collective-permute-start.15 = (bf16[4,96,1536]{2,1,0:T(8,128)(2,1)}, bf16[4,96,1536]{2,1,0:T(8,128)(2,1)}, u32[]{:S(2)}, u32[]{:S(2)}) collective-permute-start(bf16[4,96,1536]{2,1,0:T(8,128)(2,1)} %pad_maximum_fusion.2), channel_id=1, source_target_pairs={{0,12},{1,13},{2,14},{3,15},{4,0},{5,1},{6,2},{7,3},{8,4},{9,5},{1... | collective-permute-start | bytes 3538952 | tf_op jit(solution)/shard_map/ppermute | solution.py:27
  125.9 10.6 %collective-permute-start.17 = (bf16[2,96,1536]{2,1,0:T(8,128)(2,1)}, bf16[2,96,1536]{2,1,0:T(8,128)(2,1)}, u32[]{:S(2)}, u32[]{:S(2)}) collective-permute-start(bf16[2,96,1536]{2,1,0:T(8,128)(2,1)} %add_convert_fusion.3), channel_id=1, source_target_pairs={{0,4},{1,5},{2,6},{3,7},{4,8},{5,9},{6,10},{7,11},{8,12},{9,13},{1... | collective-permute-start | bytes 1769480 | tf_op jit(solution)/shard_map/ppermute | solution.py:27
  139.5 11.5 %collective-permute-start.18 = (bf16[2,96,1536]{2,1,0:T(8,128)(2,1)}, bf16[2,96,1536]{2,1,0:T(8,128)(2,1)}, u32[]{:S(2)}, u32[]{:S(2)}) collective-permute-start(bf16[2,96,1536]{2,1,0:T(8,128)(2,1)} %get-tuple-element.37), channel_id=1, source_target_pairs={{0,12},{1,13},{2,14},{3,15},{4,0},{5,1},{6,2},{7,3},{8,4},{9,5},{1... | collective-permute-start | bytes 1769480 | tf_op jit(solution)/shard_map/ppermute | solution.py:27
  141.3 9.6 %collective-permute-start.20 = (bf16[4,96,64]{2,1,0:T(8,128)(2,1)S(1)}, bf16[4,96,64]{2,1,0:T(8,128)(2,1)S(1)}, u32[]{:S(2)}, u32[]{:S(2)}) collective-permute-start(bf16[4,96,64]{2,1,0:T(8,128)(2,1)S(1)} %get-tuple-element.46), channel_id=1, source_target_pairs={{0,12},{1,13},{2,14},{3,15},{4,0},{5,1},{6,2},{7,3},{8,4},{9,5},{1... | collective-permute-start | bytes 147464 | tf_op jit(solution)/shard_map/ppermute | solution.py:27
  143.6 7.3 %collective-permute-start.19 = (bf16[4,96,64]{2,1,0:T(8,128)(2,1)S(1)}, bf16[4,96,64]{2,1,0:T(8,128)(2,1)S(1)}, u32[]{:S(2)}, u32[]{:S(2)}) collective-permute-start(bf16[4,96,64]{2,1,0:T(8,128)(2,1)S(1)} %get-tuple-element.45), channel_id=1, source_target_pairs={{0,4},{1,5},{2,6},{3,7},{4,8},{5,9},{6,10},{7,11},{8,12},{9,13},{1... | collective-permute-start | bytes 147464 | tf_op jit(solution)/shard_map/ppermute | solution.py:27
  155.8 8.2 %collective-permute-start.24 = (bf16[96,1600]{1,0:T(8,128)(2,1)}, bf16[96,1600]{1,0:T(8,128)(2,1)}, u32[]{:S(2)}, u32[]{:S(2)}) collective-permute-start(bf16[96,1600]{1,0:T(8,128)(2,1)} %get-tuple-element.34), channel_id=1, source_target_pairs={{0,16},{1,17},{2,18},{3,19},{4,20},{5,21},{6,22},{7,23},{8,24},{9,... | collective-permute-start | bytes 921608 | tf_op jit(solution)/shard_map/ppermute | solution.py:27
  157.0 8.8 %collective-permute-start.23 = (bf16[96,1600]{1,0:T(8,128)(2,1)}, bf16[96,1600]{1,0:T(8,128)(2,1)}, u32[]{:S(2)}, u32[]{:S(2)}) collective-permute-start(bf16[96,1600]{1,0:T(8,128)(2,1)} %get-tuple-element.35), channel_id=1, source_target_pairs={{0,80},{1,81},{2,82},{3,83},{4,84},{5,85},{6,86},{7,87},{8,88},{9,... | collective-permute-start | bytes 921608 | tf_op jit(solution)/shard_map/ppermute | solution.py:27
  158.2 9.0 %collective-permute-start.22 = (bf16[96,1600]{1,0:T(8,128)(2,1)}, bf16[96,1600]{1,0:T(8,128)(2,1)}, u32[]{:S(2)}, u32[]{:S(2)}) collective-permute-start(bf16[96,1600]{1,0:T(8,128)(2,1)} %get-tuple-element.33), channel_id=1, source_target_pairs={{0,64},{1,65},{2,66},{3,67},{4,68},{5,69},{6,70},{7,71},{8,72},{9,... | collective-permute-start | bytes 921608 | tf_op jit(solution)/shard_map/ppermute | solution.py:27
  168.6 7.4 %collective-permute-start.27 = (f32[24,1600]{1,0:T(8,128)S(1)}, f32[24,1600]{1,0:T(8,128)S(1)}, u32[]{:S(2)}, u32[]{:S(2)}) collective-permute-start(f32[24,1600]{1,0:T(8,128)S(1)} %get-tuple-element.41), channel_id=1, source_target_pairs={{0,2},{1,3},{2,0},{3,1},{4,6},{5,7},{6,4},{7,5},{8,10},{9,11},{10,... | collective-permute-start | bytes 460808 | tf_op jit(solution)/shard_map/ppermute | solution.py:27
  (31 other events, 193.5 us)

commit v3 on v2

--- a/solution.py
+++ b/solution.py
@@ -375,12 +375,13 @@
     if beside is not None:
         one = beside((send_f, send_b))
         got_f, got_b, one = tied((got_f, got_b, one))
-    from_a, near_b = halves(got_f)
-    from_b, near_a = halves(got_b)
+    from_a, from_b = got_f[:cut], got_b[:cut]
     sum_a = (up_a.astype(F32) + from_a.astype(F32)).astype(BF)
     sum_b = (down_b.astype(F32) + from_b.astype(F32)).astype(BF)
     last_a = hop(sum_a, forward)
     last_b = hop(sum_b, back)
+    last_a, last_b, got_f, got_b = tied((last_a, last_b, got_f, got_b))
+    near_b, near_a = got_f[cut:], got_b[cut:]
     a = own_a.astype(F32) + near_a.astype(F32) + last_a.astype(F32)
     b = own_b.astype(F32) + near_b.astype(F32) + last_b.astype(F32)
     return jnp.concatenate([a, b], axis=0), one

time: 181 us -> 171 us (0.945)
  waiting for transfers between devices: 32.1 us -> 22 us
    ppermute x22, waiting for transfers between devices: 30.4 us -> 20.1 us  [hop(): return lax.ppermute(values, AXES, pairs)]
    another operation x2 -> x1, other arithmetic: 4.52 us -> 2.03 us
    convert_element_type x0 -> x1, other arithmetic: none -> 2.05 us  [ring_reduce(): sum_b = (down_b.astype(F32) + from_b.astype(F32)).astype(BF)]
    unnamed x53 -> x49, local copies, waits for them, and re-layouts: 6.8 us -> 6.78 us
  transfers between devices with their start and end apart: 29 -> 29, of which waited for: 11 -> 10; matrix products, arithmetic and copies ran while one was open for 13% -> 16% of each run, Pallas kernels for 27% -> 28%
where the time goes in v3:
time: 171 us; the launch traced here: 169 us
  starting transfers between devices  55.4 us (32%)
  Pallas kernels  48.1 us (28%)
  waiting for transfers between devices  22 us (13%)
  other arithmetic  21.1 us (12%)
  local copies, waits for them, and re-layouts  14.3 us (8%)
  matrix products  7.32 us (4%)
    ppermute x22, starting transfers between devices, hop(): return lax.ppermute(values, AXES, pairs)  33.8 us
    ppermute x22, waiting for transfers between devices, hop(): return lax.ppermute(values, AXES, pairs)  20.1 us
    pallas_call x1, Pallas kernels, backward_call(): pl.pallas_call(backward_kernel, grid_spec=pltpu.PrefetchScalarGridSpec(nu...  13.3 us
    pallas_call x2, Pallas kernels, values_call(): pl.pallas_call(values_kernel, grid_spec=pltpu.PrefetchScalarGridSpec(num_...  11.2 us
    ppermute x4, starting transfers between devices, swap(): return lax.ppermute(x, axis, [(0, 1), (1, 0)])  11.1 us
    pallas_call x2, Pallas kernels, conv_clips(): pl.pallas_call(conv_kernel, grid=(clips // step,), out_shape=jax.ShapeDty...  8.43 us
    dot_general x1, matrix products, local(): lax.dot_general(mod_rows, cot_both, (((0,), (0,)), ((), ())), preferred_e...  7.32 us
    pallas_call x1, Pallas kernels, place(): pl.pallas_call(place_kernel, out_shape=jax.ShapeDtypeStruct((2, 4, 4, row...  6.82 us
  transfers between devices with their start and end apart: 29, of which 10 were waited for; matrix products, arithmetic and copies ran while one was open for 16% of the time, Pallas kernels for 28%

profile of v3, /device:TPU:1, one launch (start us, length us, event | category | flops | bytes accessed | tf_op | source)
XLA Modules:
  0.0 169.4 jit_solution(31045258110535949)
XLA Ops:
  2.3 4.6 %collective-permute-start.1 = (bf16[96,768]{1,0:T(8,128)(2,1)}, bf16[96,768]{1,0:T(8,128)(2,1)}, u32[]{:S(2)}, u32[]{:S(2)}) collective-permute-start(bf16[96,768]{1,0:T(8,128)(2,1)} %constant_dynamic-slice_fusion), channel_id=1, source_target_pairs={{0,80},{1,81},{2,82},{3,83},{4,84},{5,85},{6,86},{7,87},{8,88},{9,... | collective-permute-start | bytes 442376 | tf_op jit(solution)/shard_map/ppermute | solution.py:27
  11.0 2.3 %collective-permute-start = (bf16[16,2,32,512]{3,2,1,0:T(8,128)(2,1)S(1)}, bf16[16,2,32,512]{3,2,1,0:T(8,128)(2,1)}, u32[]{:S(2)}, u32[]{:S(2)}) collective-permute-start(bf16[16,2,32,512]{3,2,1,0:T(8,128)(2,1)S(1)} %fusion.9.normed), channel_id=1, source_target_pairs={{0,32},{32,64},{64,96},{1,33},{33,65},{65,97},{2,34},{34,66},{66,9... | collective-permute-start | bytes 3145736 | tf_op jit(solution)/shard_map/ppermute | solution.py:450
  22.4 2.7 %collective-permute-start.7 = (bf16[2,2,96,768]{3,2,1,0:T(8,128)(2,1)}, bf16[2,2,96,768]{3,2,1,0:T(8,128)(2,1)}, u32[]{:S(2)}, u32[]{:S(2)}) collective-permute-start(bf16[2,2,96,768]{3,2,1,0:T(8,128)(2,1)} %pad_maximum_fusion.4.own), channel_id=1, source_target_pairs={{0,12},{1,13},{2,14},{3,15},{4,8},{5,9},{6,10},{7,11},{8,4},{9,5},... | collective-permute-start | bytes 1769480 | tf_op jit(solution)/shard_map/ppermute | solution.py:27
  26.6 7.5 %collective-permute-done.7.own2 = bf16[2,2,96,768]{3,2,1,0:T(8,128)(2,1)} collective-permute-done((bf16[2,2,96,768]{3,2,1,0:T(8,128)(2,1)}, bf16[2,2,96,768]{3,2,1,0:T(8,128)(2,1)}, u32[]{:S(2)}, u32[]{:S(2)}) %collective-permute-start.7) | collective-permute-done | bytes 589856 | tf_op jit(solution)/shard_map/ppermute | solution.py:27
  34.0 4.8 %collective-permute-start.9 = (bf16[2,2,96,768]{3,2,1,0:T(8,128)(2,1)}, bf16[2,2,96,768]{3,2,1,0:T(8,128)(2,1)}, u32[]{:S(2)}, u32[]{:S(2)}) collective-permute-start(bf16[2,2,96,768]{3,2,1,0:T(8,128)(2,1)} %collective-permute-done.7.own2), channel_id=1, source_target_pairs={{0,3},{1,0},{2,1},{3,2},{4,7},{5,4},{6,5},{7,6},{8,11},{9,8},{10,9... | collective-permute-start | bytes 1769480 | tf_op jit(solution)/shard_map/ppermute | solution.py:27
  38.8 4.1 %conv.2 = bf16[16,2,32,16]{3,2,1,0:T(8,128)(2,1)S(1)} custom-call(bf16[32,2,32,512]{3,2,1,0:T(8,128)(2,1)S(1)} %copy-done.2, bf16[16,2,32,512]{3,2,1,0:T(8,128)(2,1)} %collective-permute-done.before, bf16[16,2,32,512]{3,2,1,0:T(8,128)(2,1)S(1)} %fusion.9.normed, bf16[3,512,512]{2,1,0:T(8,128)(2,1)} %bitcast.100, bf16[512,16]{1,0:T(8,128)(2,1)S(1)} %copy-done.5), custom_call_target="tpu_custom_call" | custom-call | flops 1610612736 | bytes 4194304 | tf_op jit(solution)/shard_map/conv/pallas_call | solution.py:140
  43.2 4.3 %conv.3 = bf16[16,2,32,16]{3,2,1,0:T(8,128)(2,1)S(1)} custom-call(bf16[32,2,32,512]{3,2,1,0:T(8,128)(2,1)S(1)} %copy-done.2, bf16[16,2,32,512]{3,2,1,0:T(8,128)(2,1)} %collective-permute-done.2.before, bf16[16,2,32,512]{3,2,1,0:T(8,128)(2,1)} %fusion.13.normed, bf16[3,512,512]{2,1,0:T(8,128)(2,1)} %bitcast.101, bf16[512,16]{1,0:T(8,128)(2,1)S(1)} %copy-done.5), custom_call_target="tpu_custom_call" | custom-call | flops 1610612736 | bytes 4194304 | tf_op jit(solution)/shard_map/conv/pallas_call | solution.py:140
  49.5 6.1 %all-to-all-start = ((bf16[32,56,128]{2,1,0:T(8,128)(2,1)}), bf16[32,56,128]{2,1,0:T(8,128)(2,1)S(1)}, u32[]{:S(2)}, u32[]{:S(2)}) async-start(bf16[32,56,128]{2,1,0:T(8,128)(2,1)} %pad_maximum_fusion.5), calls=%async_computation | async-start | bytes 917504 | tf_op jit(solution)/shard_map/all_to_all | solution.py:353
  55.7 2.5 %collective-permute-start.5 = (bf16[2,2,96,768]{3,2,1,0:T(8,128)(2,1)}, bf16[2,2,96,768]{3,2,1,0:T(8,128)(2,1)S(1)}, u32[]{:S(2)}, u32[]{:S(2)}) collective-permute-start(bf16[2,2,96,768]{3,2,1,0:T(8,128)(2,1)} %pad_maximum_fusion.4.own), channel_id=1, source_target_pairs={{0,3},{1,0},{2,1},{3,2},{4,7},{5,4},{6,5},{7,6},{8,11},{9,8},{10,9... | collective-permute-start | bytes 1769480 | tf_op jit(solution)/shard_map/ppermute | solution.py:27
  58.2 3.5 %collective-permute-start.13 = (bf16[512,1536]{1,0:T(8,128)(2,1)}, bf16[512,1536]{1,0:T(8,128)(2,1)}, u32[]{:S(2)}, u32[]{:S(2)}) collective-permute-start(bf16[512,1536]{1,0:T(8,128)(2,1)} %bitcast.15.x), channel_id=1, source_target_pairs={{0,32},{32,0},{1,33},{33,1},{2,34},{34,2},{3,35},{35,3},{4,36},{36... | collective-permute-start | bytes 4718600 | tf_op jit(solution)/shard_map/ppermute | solution.py:45
  67.7 4.4 %shard_map.130 = (bf16[512,3072]{1,0:T(8,128)(2,1)}, bf16[512,1536]{1,0:T(8,128)(2,1)S(1)}, bf16[512,1536]{1,0:T(8,128)(2,1)}) custom-call(s32[1]{0:T(128)} %bitcast.idx, bf16[512,64]{1,0:T(8,128)(2,1)S(1)} %bitcast.96, bf16[3072,64]{1,0:T(8,128)(2,1)S(1)} %bitcast.94, f32[1,3072]{1,0:T(1,128)S(1)} %copy-done.8, f32[1,3072]{1,0:T(1,128)S(1)} %copy-done.9), custom_call_target="tpu_custom_call" | custom-call | flops 1610612736 | bytes 16777216 | tf_op jit(solution)/shard_map/pallas_call | solution.py:331
  73.3 4.6 %collective-permute-start.12 = (bf16[512,1536]{1,0:T(8,128)(2,1)}, bf16[512,1536]{1,0:T(8,128)(2,1)}, u32[]{:S(2)}, u32[]{:S(2)}) collective-permute-start(bf16[512,1536]{1,0:T(8,128)(2,1)} %get-tuple-element.25), channel_id=1, source_target_pairs={{0,32},{32,0},{1,33},{33,1},{2,34},{34,2},{3,35},{35,3},{4,36},{36... | collective-permute-start | bytes 4718600 | tf_op jit(solution)/shard_map/ppermute | solution.py:45
  78.5 6.8 %place.1 = bf16[2,4,4,96,768]{4,3,2,1,0:T(8,128)(2,1)} custom-call(s32[4]{0:T(128)S(1)} %pad_add_fusion.idx, bf16[2,2,96,768]{3,2,1,0:T(8,128)(2,1)} %pad_maximum_fusion.4.own, bf16[2,2,96,768]{3,2,1,0:T(8,128)(2,1)} %collective-permute-done.4.up, bf16[2,2,96,768]{3,2,1,0:T(8,128)(2,1)S(1)} %collective-permute-done.5.down, ...), custom_call_target="tpu_custom_call" | custom-call | bytes 9437184 | tf_op jit(solution)/shard_map/place/pallas_call | solution.py:86
  87.4 4.0 %flip.1.cot_t = bf16[1536,512]{1,0:T(8,128)(2,1)} custom-call(bf16[512,1536]{1,0:T(8,128)(2,1)} %bitcast.15.x), custom_call_target="tpu_custom_call" | custom-call | bytes 3145728 | tf_op jit(solution)/shard_map/flip/pallas_call | solution.py:109
  91.4 7.3 %convolution_convert_fusion = bf16[1536,1536]{1,0:T(8,128)(2,1)S(1)} fusion(bf16[512,1536]{1,0:T(8,128)(2,1)} %collective-permute-done.12, bf16[512,1536]{1,0:T(8,128)(2,1)S(1)} %copy-done.11, bf16[512,1536]{1,0:T(8,128)(2,1)} %collective-permute-done.13, bf16[512,1536]{1,0:T(8,128)(2,1)} %bitcast.15.x), kind=kOutput, calls=%fused_computation.1 | convolution fusion | flops 4846780416 | bytes 11010048 | tf_op jit(solution)/shard_map/dot_general | solution.py:507
  103.6 2.7 %collective-permute-start.15 = (bf16[4,96,1536]{2,1,0:T(8,128)(2,1)}, bf16[4,96,1536]{2,1,0:T(8,128)(2,1)}, u32[]{:S(2)}, u32[]{:S(2)}) collective-permute-start(bf16[4,96,1536]{2,1,0:T(8,128)(2,1)} %pad_maximum_fusion.2), channel_id=1, source_target_pairs={{0,12},{1,13},{2,14},{3,15},{4,0},{5,1},{6,2},{7,3},{8,4},{9,5},{1... | collective-permute-start | bytes 3538952 | tf_op jit(solution)/shard_map/ppermute | solution.py:27
  108.0 13.3 %backward.1 = f32[3072,64]{1,0:T(8,128)S(1)} custom-call(s32[1]{0:T(128)} %bitcast.idx, bf16[64,512]{1,0:T(8,128)(2,1)S(1)} %copy.30.tok_t, bf16[512,64]{1,0:T(8,128)(2,1)S(1)} %bitcast.98, bf16[3072,64]{1,0:T(8,128)(2,1)S(1)} %bitcast.95, f32[3072,128]{1,0:T(8,128)S(1)} %broadcast_in_dim.35.scaling, bf16[1536,512]{1,0:T(8,128)(2,1)S(1)} %copy-done.4, ...), custom_call_target="tpu_custom_call" | custom-call | flops 4831838208 | bytes 16777216 | tf_op jit(solution)/shard_map/backward/pallas_call | solution.py:254
  124.5 2.4 %add_convert_fusion.3 = bf16[2,96,1536]{2,1,0:T(8,128)(2,1)} fusion(bf16[4,96,1536]{2,1,0:T(8,128)(2,1)} %copy-done.15, bf16[4,96,1536]{2,1,0:T(8,128)(2,1)} %collective-permute-done.14), kind=kLoop, calls=%fused_computation.30 | loop fusion | flops 1179648 | bytes 1769472 | tf_op jit(solution)/shard_map/convert_element_type | solution.py:379
  128.9 2.7 %collective-permute-start.18 = (bf16[2,96,1536]{2,1,0:T(8,128)(2,1)}, bf16[2,96,1536]{2,1,0:T(8,128)(2,1)}, u32[]{:S(2)}, u32[]{:S(2)}) collective-permute-start(bf16[2,96,1536]{2,1,0:T(8,128)(2,1)} %add_convert_fusion.2), channel_id=1, source_target_pairs={{0,12},{1,13},{2,14},{3,15},{4,0},{5,1},{6,2},{7,3},{8,4},{9,5},{1... | collective-permute-start | bytes 1769480 | tf_op jit(solution)/shard_map/ppermute | solution.py:27
  135.8 2.6 %collective-permute-done.21 = bf16[4,96,64]{2,1,0:T(8,128)(2,1)S(1)} collective-permute-done((bf16[4,96,64]{2,1,0:T(8,128)(2,1)S(1)}, bf16[4,96,64]{2,1,0:T(8,128)(2,1)S(1)}, u32[]{:S(2)}, u32[]{:S(2)}) %collective-permute-start.21) | collective-permute-done | bytes 49184 | tf_op jit(solution)/shard_map/ppermute | solution.py:27
  138.4 2.8 %collective-permute-done.20 = bf16[4,96,64]{2,1,0:T(8,128)(2,1)S(1)} collective-permute-done((bf16[4,96,64]{2,1,0:T(8,128)(2,1)S(1)}, bf16[4,96,64]{2,1,0:T(8,128)(2,1)S(1)}, u32[]{:S(2)}, u32[]{:S(2)}) %collective-permute-start.20) | collective-permute-done | bytes 49184 | tf_op jit(solution)/shard_map/ppermute | solution.py:27
  148.0 5.6 %values.2.rest_0_ = bf16[512,1536]{1,0:T(8,128)(2,1)} custom-call(s32[1]{0:T(128)} %bitcast.idx, bf16[512,3072]{1,0:T(8,128)(2,1)S(1)} %copy-done.3, bf16[3072,768]{1,0:T(8,128)(2,1)} %bitcast.13.weight.w_kept), custom_call_target="tpu_custom_call" | custom-call | flops 2415919104 | bytes 7340032 | tf_op jit(solution)/shard_map/values/pallas_call | solution.py:298
  160.2 5.6 %values.3 = bf16[512,1536]{1,0:T(8,128)(2,1)} custom-call(s32[1]{0:T(128)S(6)} %sub.27.idx, bf16[512,3072]{1,0:T(8,128)(2,1)S(1)} %copy-done.3, bf16[3072,768]{1,0:T(8,128)(2,1)} %collective-permute-done.11.weight.w_got, bf16[512,1536]{1,0:T(8,128)(2,1)} %values.2.rest_0_), custom_call_target="tpu_custom_call", output_to_operand_aliasing={{}: (3, {})} | custom-call | flops 2415919104 | bytes 7340032 | tf_op jit(solution)/shard_map/values/pallas_call | solution.py:298
  165.8 2.3 %collective-permute-done.25 = f32[24,1600]{1,0:T(8,128)S(1)} collective-permute-done((f32[24,1600]{1,0:T(8,128)S(1)}, f32[24,1600]{1,0:T(8,128)S(1)}, u32[]{:S(2)}, u32[]{:S(2)}) %collective-permute-start.25) | collective-permute-done | bytes 153632 | tf_op jit(solution)/shard_map/ppermute | solution.py:27
  (150 shorter events, 58.9 us)
Async XLA Ops:
  2.3 12.1 %collective-permute-start.1 = (bf16[96,768]{1,0:T(8,128)(2,1)}, bf16[96,768]{1,0:T(8,128)(2,1)}, u32[]{:S(2)}, u32[]{:S(2)}) collective-permute-start(bf16[96,768]{1,0:T(8,128)(2,1)} %constant_dynamic-slice_fusion), channel_id=1, source_target_pairs={{0,80},{1,81},{2,82},{3,83},{4,84},{5,85},{6,86},{7,87},{8,88},{9,... | collective-permute-start | bytes 442376 | tf_op jit(solution)/shard_map/ppermute | solution.py:27
  11.0 27.7 %collective-permute-start = (bf16[16,2,32,512]{3,2,1,0:T(8,128)(2,1)S(1)}, bf16[16,2,32,512]{3,2,1,0:T(8,128)(2,1)}, u32[]{:S(2)}, u32[]{:S(2)}) collective-permute-start(bf16[16,2,32,512]{3,2,1,0:T(8,128)(2,1)S(1)} %fusion.9.normed), channel_id=1, source_target_pairs={{0,32},{32,64},{64,96},{1,33},{33,65},{65,97},{2,34},{34,66},{66,9... | collective-permute-start | bytes 3145736 | tf_op jit(solution)/shard_map/ppermute | solution.py:450
  18.4 24.8 %collective-permute-start.2 = (bf16[16,2,32,512]{3,2,1,0:T(8,128)(2,1)}, bf16[16,2,32,512]{3,2,1,0:T(8,128)(2,1)}, u32[]{:S(2)}, u32[]{:S(2)}) collective-permute-start(bf16[16,2,32,512]{3,2,1,0:T(8,128)(2,1)} %fusion.13.normed), channel_id=1, source_target_pairs={{0,32},{32,64},{64,96},{1,33},{33,65},{65,97},{2,34},{34,66},{66,9... | collective-permute-start | bytes 3145736 | tf_op jit(solution)/shard_map/ppermute | solution.py:450
  22.4 11.6 %collective-permute-start.7 = (bf16[2,2,96,768]{3,2,1,0:T(8,128)(2,1)}, bf16[2,2,96,768]{3,2,1,0:T(8,128)(2,1)}, u32[]{:S(2)}, u32[]{:S(2)}) collective-permute-start(bf16[2,2,96,768]{3,2,1,0:T(8,128)(2,1)} %pad_maximum_fusion.4.own), channel_id=1, source_target_pairs={{0,12},{1,13},{2,14},{3,15},{4,8},{5,9},{6,10},{7,11},{8,4},{9,5},... | collective-permute-start | bytes 1769480 | tf_op jit(solution)/shard_map/ppermute | solution.py:27
  25.3 37.6 %collective-permute-start.4 = (bf16[2,2,96,768]{3,2,1,0:T(8,128)(2,1)}, bf16[2,2,96,768]{3,2,1,0:T(8,128)(2,1)}, u32[]{:S(2)}, u32[]{:S(2)}) collective-permute-start(bf16[2,2,96,768]{3,2,1,0:T(8,128)(2,1)} %pad_maximum_fusion.4.own), channel_id=1, source_target_pairs={{0,1},{1,2},{2,3},{3,0},{4,5},{5,6},{6,7},{7,4},{8,9},{9,10},{10,1... | collective-permute-start | bytes 1769480 | tf_op jit(solution)/shard_map/ppermute | solution.py:27
  34.0 30.1 %collective-permute-start.9 = (bf16[2,2,96,768]{3,2,1,0:T(8,128)(2,1)}, bf16[2,2,96,768]{3,2,1,0:T(8,128)(2,1)}, u32[]{:S(2)}, u32[]{:S(2)}) collective-permute-start(bf16[2,2,96,768]{3,2,1,0:T(8,128)(2,1)} %collective-permute-done.7.own2), channel_id=1, source_target_pairs={{0,3},{1,0},{2,1},{3,2},{4,7},{5,4},{6,5},{7,6},{8,11},{9,8},{10,9... | collective-permute-start | bytes 1769480 | tf_op jit(solution)/shard_map/ppermute | solution.py:27
  49.5 16.4 %all-to-all-start = ((bf16[32,56,128]{2,1,0:T(8,128)(2,1)}), bf16[32,56,128]{2,1,0:T(8,128)(2,1)S(1)}, u32[]{:S(2)}, u32[]{:S(2)}) async-start(bf16[32,56,128]{2,1,0:T(8,128)(2,1)} %pad_maximum_fusion.5), calls=%async_computation | async-start | bytes 917504 | tf_op jit(solution)/shard_map/all_to_all | solution.py:353
  55.7 17.6 %collective-permute-start.5 = (bf16[2,2,96,768]{3,2,1,0:T(8,128)(2,1)}, bf16[2,2,96,768]{3,2,1,0:T(8,128)(2,1)S(1)}, u32[]{:S(2)}, u32[]{:S(2)}) collective-permute-start(bf16[2,2,96,768]{3,2,1,0:T(8,128)(2,1)} %pad_maximum_fusion.4.own), channel_id=1, source_target_pairs={{0,3},{1,0},{2,1},{3,2},{4,7},{5,4},{6,5},{7,6},{8,11},{9,8},{10,9... | collective-permute-start | bytes 1769480 | tf_op jit(solution)/shard_map/ppermute | solution.py:27
  58.2 33.2 %collective-permute-start.13 = (bf16[512,1536]{1,0:T(8,128)(2,1)}, bf16[512,1536]{1,0:T(8,128)(2,1)}, u32[]{:S(2)}, u32[]{:S(2)}) collective-permute-start(bf16[512,1536]{1,0:T(8,128)(2,1)} %bitcast.15.x), channel_id=1, source_target_pairs={{0,32},{32,0},{1,33},{33,1},{2,34},{34,2},{3,35},{35,3},{4,36},{36... | collective-permute-start | bytes 4718600 | tf_op jit(solution)/shard_map/ppermute | solution.py:45
  61.7 16.8 %collective-permute-start.8 = (bf16[2,2,96,768]{3,2,1,0:T(8,128)(2,1)}, bf16[2,2,96,768]{3,2,1,0:T(8,128)(2,1)S(1)}, u32[]{:S(2)}, u32[]{:S(2)}) collective-permute-start(bf16[2,2,96,768]{3,2,1,0:T(8,128)(2,1)} %collective-permute-done.7.own2), channel_id=1, source_target_pairs={{0,1},{1,2},{2,3},{3,0},{4,5},{5,6},{6,7},{7,4},{8,9},{9,10},{10,1... | collective-permute-start | bytes 1769480 | tf_op jit(solution)/shard_map/ppermute | solution.py:27
  62.9 15.6 %collective-permute-start.6 = (bf16[2,2,96,768]{3,2,1,0:T(8,128)(2,1)}, bf16[2,2,96,768]{3,2,1,0:T(8,128)(2,1)S(1)}, u32[]{:S(2)}, u32[]{:S(2)}) collective-permute-start(bf16[2,2,96,768]{3,2,1,0:T(8,128)(2,1)} %collective-permute-done.4.up), channel_id=1, source_target_pairs={{0,1},{1,2},{2,3},{3,0},{4,5},{5,6},{6,7},{7,4},{8,9},{9,10},{10,1... | collective-permute-start | bytes 1769480 | tf_op jit(solution)/shard_map/ppermute | solution.py:27
  64.1 14.4 %collective-permute-start.10 = (bf16[2,2,96,768]{3,2,1,0:T(8,128)(2,1)}, bf16[2,2,96,768]{3,2,1,0:T(8,128)(2,1)S(1)}, u32[]{:S(2)}, u32[]{:S(2)}) collective-permute-start(bf16[2,2,96,768]{3,2,1,0:T(8,128)(2,1)} %collective-permute-done.9.down2), channel_id=1, source_target_pairs={{0,3},{1,0},{2,1},{3,2},{4,7},{5,4},{6,5},{7,6},{8,11},{9,8},{10,9... | collective-permute-start | bytes 1769480 | tf_op jit(solution)/shard_map/ppermute | solution.py:27
  73.3 18.1 %collective-permute-start.12 = (bf16[512,1536]{1,0:T(8,128)(2,1)}, bf16[512,1536]{1,0:T(8,128)(2,1)}, u32[]{:S(2)}, u32[]{:S(2)}) collective-permute-start(bf16[512,1536]{1,0:T(8,128)(2,1)} %get-tuple-element.25), channel_id=1, source_target_pairs={{0,32},{32,0},{1,33},{33,1},{2,34},{34,2},{3,35},{35,3},{4,36},{36... | collective-permute-start | bytes 4718600 | tf_op jit(solution)/shard_map/ppermute | solution.py:45
  85.3 21.1 %collective-permute-start.11 = (bf16[3072,768]{1,0:T(8,128)(2,1)}, bf16[3072,768]{1,0:T(8,128)(2,1)}, u32[]{:S(2)}, u32[]{:S(2)}) collective-permute-start(bf16[3072,768]{1,0:T(8,128)(2,1)} %bitcast.13.weight.w_kept), channel_id=1, source_target_pairs={{0,32},{32,0},{1,33},{33,1},{2,34},{34,2},{3,35},{35,3},{4,36},{36... | collective-permute-start | bytes 14155784 | tf_op jit(solution)/shard_map/ppermute | solution.py:45
  102.4 20.5 %collective-permute-start.14 = (bf16[4,96,1536]{2,1,0:T(8,128)(2,1)}, bf16[4,96,1536]{2,1,0:T(8,128)(2,1)}, u32[]{:S(2)}, u32[]{:S(2)}) collective-permute-start(bf16[4,96,1536]{2,1,0:T(8,128)(2,1)} %pad_maximum_fusion.1), channel_id=1, source_target_pairs={{0,4},{1,5},{2,6},{3,7},{4,8},{5,9},{6,10},{7,11},{8,12},{9,13},{1... | collective-permute-start | bytes 3538952 | tf_op jit(solution)/shard_map/ppermute | solution.py:27
  103.6 19.3 %collective-permute-start.15 = (bf16[4,96,1536]{2,1,0:T(8,128)(2,1)}, bf16[4,96,1536]{2,1,0:T(8,128)(2,1)}, u32[]{:S(2)}, u32[]{:S(2)}) collective-permute-start(bf16[4,96,1536]{2,1,0:T(8,128)(2,1)} %pad_maximum_fusion.2), channel_id=1, source_target_pairs={{0,12},{1,13},{2,14},{3,15},{4,0},{5,1},{6,2},{7,3},{8,4},{9,5},{1... | collective-permute-start | bytes 3538952 | tf_op jit(solution)/shard_map/ppermute | solution.py:27
  126.8 14.5 %collective-permute-start.17 = (bf16[2,96,1536]{2,1,0:T(8,128)(2,1)}, bf16[2,96,1536]{2,1,0:T(8,128)(2,1)}, u32[]{:S(2)}, u32[]{:S(2)}) collective-permute-start(bf16[2,96,1536]{2,1,0:T(8,128)(2,1)} %add_convert_fusion.3), channel_id=1, source_target_pairs={{0,4},{1,5},{2,6},{3,7},{4,8},{5,9},{6,10},{7,11},{8,12},{9,13},{1... | collective-permute-start | bytes 1769480 | tf_op jit(solution)/shard_map/ppermute | solution.py:27
  128.9 12.5 %collective-permute-start.18 = (bf16[2,96,1536]{2,1,0:T(8,128)(2,1)}, bf16[2,96,1536]{2,1,0:T(8,128)(2,1)}, u32[]{:S(2)}, u32[]{:S(2)}) collective-permute-start(bf16[2,96,1536]{2,1,0:T(8,128)(2,1)} %add_convert_fusion.2), channel_id=1, source_target_pairs={{0,12},{1,13},{2,14},{3,15},{4,0},{5,1},{6,2},{7,3},{8,4},{9,5},{1... | collective-permute-start | bytes 1769480 | tf_op jit(solution)/shard_map/ppermute | solution.py:27
  145.5 8.0 %collective-permute-start.24 = (bf16[96,1600]{1,0:T(8,128)(2,1)}, bf16[96,1600]{1,0:T(8,128)(2,1)}, u32[]{:S(2)}, u32[]{:S(2)}) collective-permute-start(bf16[96,1600]{1,0:T(8,128)(2,1)} %get-tuple-element.42), channel_id=1, source_target_pairs={{0,16},{1,17},{2,18},{3,19},{4,20},{5,21},{6,22},{7,23},{8,24},{9,... | collective-permute-start | bytes 921608 | tf_op jit(solution)/shard_map/ppermute | solution.py:27
  146.5 8.8 %collective-permute-start.23 = (bf16[96,1600]{1,0:T(8,128)(2,1)}, bf16[96,1600]{1,0:T(8,128)(2,1)}, u32[]{:S(2)}, u32[]{:S(2)}) collective-permute-start(bf16[96,1600]{1,0:T(8,128)(2,1)} %get-tuple-element.43), channel_id=1, source_target_pairs={{0,80},{1,81},{2,82},{3,83},{4,84},{5,85},{6,86},{7,87},{8,88},{9,... | collective-permute-start | bytes 921608 | tf_op jit(solution)/shard_map/ppermute | solution.py:27
  147.7 9.2 %collective-permute-start.22 = (bf16[96,1600]{1,0:T(8,128)(2,1)}, bf16[96,1600]{1,0:T(8,128)(2,1)}, u32[]{:S(2)}, u32[]{:S(2)}) collective-permute-start(bf16[96,1600]{1,0:T(8,128)(2,1)} %get-tuple-element.41), channel_id=1, source_target_pairs={{0,64},{1,65},{2,66},{3,67},{4,68},{5,69},{6,70},{7,71},{8,72},{9,... | collective-permute-start | bytes 921608 | tf_op jit(solution)/shard_map/ppermute | solution.py:27
  158.4 7.4 %collective-permute-start.27 = (f32[24,1600]{1,0:T(8,128)S(1)}, f32[24,1600]{1,0:T(8,128)S(1)}, u32[]{:S(2)}, u32[]{:S(2)}) collective-permute-start(f32[24,1600]{1,0:T(8,128)S(1)} %get-tuple-element.49), channel_id=1, source_target_pairs={{0,2},{1,3},{2,0},{3,1},{4,6},{5,7},{6,4},{7,5},{8,10},{9,11},{10,... | collective-permute-start | bytes 460808 | tf_op jit(solution)/shard_map/ppermute | solution.py:27
  158.7 7.1 %collective-permute-start.26 = (f32[24,1600]{1,0:T(8,128)S(1)}, f32[24,1600]{1,0:T(8,128)S(1)}, u32[]{:S(2)}, u32[]{:S(2)}) collective-permute-start(f32[24,1600]{1,0:T(8,128)S(1)} %get-tuple-element.50), channel_id=1, source_target_pairs={{0,3},{1,0},{2,1},{3,2},{4,7},{5,4},{6,5},{7,6},{8,11},{9,8},{10,9... | collective-permute-start | bytes 460808 | tf_op jit(solution)/shard_map/ppermute | solution.py:27
  159.9 8.2 %collective-permute-start.25 = (f32[24,1600]{1,0:T(8,128)S(1)}, f32[24,1600]{1,0:T(8,128)S(1)}, u32[]{:S(2)}, u32[]{:S(2)}) collective-permute-start(f32[24,1600]{1,0:T(8,128)S(1)} %get-tuple-element.48), channel_id=1, source_target_pairs={{0,1},{1,2},{2,3},{3,0},{4,5},{5,6},{6,7},{7,4},{8,9},{9,10},{10,1... | collective-permute-start | bytes 460808 | tf_op jit(solution)/shard_map/ppermute | solution.py:27
  (29 other events, 169.2 us)

commit v4 on v3

--- a/solution.py
+++ b/solution.py
@@ -387,11 +387,17 @@
     return jnp.concatenate([a, b], axis=0), one
 
 
-def direct_reduce(part, dest):
-    total = part(0).astype(F32)
+def direct_pieces(part, dest):
+    pieces = [part(0)]
     for d in (1, 3, 2):
-        got = hop(part(d), dest(d))
-        total = total + got.astype(F32)
+        pieces.append(hop(part(d), dest(d)))
+    return pieces
+
+
+def add_up(pieces):
+    total = pieces[0].astype(F32)
+    for piece in pieces[1:]:
+        total = total + piece.astype(F32)
     return total
 
 
@@ -538,20 +544,19 @@
         lambda d: cut(blocks_w, d), 2, forward, back, embed_gradient
     )
     grad_e = (pick(grad_e, c, 1) + given_e.astype(F32)).astype(BF).reshape(4, 4, 96, -1)
-    chunk_e = direct_reduce(
-        lambda d: cut(grad_e, d), lambda d: by_core(along("x", d), along("z", d))
+    chunk_e = add_up(
+        direct_pieces(lambda d: cut(grad_e, d), lambda d: by_core(along("x", d), along("z", d)))
     )
     chunk = jnp.concatenate([chunk.astype(BF), chunk_e.astype(BF)], axis=-1)
 
     def second(d):
         return pick(chunk, jnp.where(c == 0, z_at(d), x_at(d)), 0)
 
-    rows = direct_reduce(second, lambda d: by_core(along("z", d), along("x", d)))
+    rows = add_up(direct_pieces(second, lambda d: by_core(along("z", d), along("x", d))))
     rows = rows.reshape(4, 24, -1)
-    summed = direct_reduce(lambda d: pick(rows, (pos["y"] + d) % 4, 0), lambda d: along("y", d))
-    grad_value = summed[:, :cols]
-    grad_embed = summed[:, cols:]
-
+    last = direct_pieces(lambda d: pick(rows, (pos["y"] + d) % 4, 0), lambda d: along("y", d))
+    grad_value = add_up([piece[:, :cols] for piece in last])
+    grad_embed = add_up([piece[:, cols:] for piece in last])
     return (projected.reshape(value_cotangent.shape), grad_value, grad_embed)
 
 

time: 171 us -> 171 us (level)
  no operation moved by 1% of the time
where the time goes in v4:
time: 171 us; the launch traced here: 169 us
  starting transfers between devices  55.4 us (32%)
  Pallas kernels  48.1 us (28%)
  other arithmetic  22.4 us (13%)
  waiting for transfers between devices  22 us (13%)
  local copies, waits for them, and re-layouts  13 us (8%)
  matrix products  7.32 us (4%)
    ppermute x22, starting transfers between devices, hop(): return lax.ppermute(values, AXES, pairs)  33.8 us
    ppermute x22, waiting for transfers between devices, hop(): return lax.ppermute(values, AXES, pairs)  20.1 us
    pallas_call x1, Pallas kernels, backward_call(): pl.pallas_call(backward_kernel, grid_spec=pltpu.PrefetchScalarGridSpec(nu...  13.3 us
    pallas_call x2, Pallas kernels, values_call(): pl.pallas_call(values_kernel, grid_spec=pltpu.PrefetchScalarGridSpec(num_...  11.2 us
    ppermute x4, starting transfers between devices, swap(): return lax.ppermute(x, axis, [(0, 1), (1, 0)])  11.1 us
    pallas_call x2, Pallas kernels, conv_clips(): pl.pallas_call(conv_kernel, grid=(clips // step,), out_shape=jax.ShapeDty...  8.43 us
    dot_general x1, matrix products, local(): lax.dot_general(mod_rows, cot_both, (((0,), (0,)), ((), ())), preferred_e...  7.32 us
    pallas_call x1, Pallas kernels, place(): pl.pallas_call(place_kernel, out_shape=jax.ShapeDtypeStruct((2, 4, 4, row...  6.82 us
  transfers between devices with their start and end apart: 29, of which 10 were waited for; matrix products, arithmetic and copies ran while one was open for 16% of the time, Pallas kernels for 28%

profile of v4, /device:TPU:1, one launch (start us, length us, event | category | flops | bytes accessed | tf_op | source)
XLA Modules:
  0.0 169.4 jit_solution(115721984033644492)
XLA Ops:
  2.3 4.6 %collective-permute-start.1 = (bf16[96,768]{1,0:T(8,128)(2,1)}, bf16[96,768]{1,0:T(8,128)(2,1)}, u32[]{:S(2)}, u32[]{:S(2)}) collective-permute-start(bf16[96,768]{1,0:T(8,128)(2,1)} %constant_dynamic-slice_fusion), channel_id=1, source_target_pairs={{0,80},{1,81},{2,82},{3,83},{4,84},{5,85},{6,86},{7,87},{8,88},{9,... | collective-permute-start | bytes 442376 | tf_op jit(solution)/shard_map/ppermute | solution.py:27
  11.0 2.3 %collective-permute-start = (bf16[16,2,32,512]{3,2,1,0:T(8,128)(2,1)S(1)}, bf16[16,2,32,512]{3,2,1,0:T(8,128)(2,1)}, u32[]{:S(2)}, u32[]{:S(2)}) collective-permute-start(bf16[16,2,32,512]{3,2,1,0:T(8,128)(2,1)S(1)} %fusion.9.normed), channel_id=1, source_target_pairs={{0,32},{32,64},{64,96},{1,33},{33,65},{65,97},{2,34},{34,66},{66,9... | collective-permute-start | bytes 3145736 | tf_op jit(solution)/shard_map/ppermute | solution.py:456
  22.4 2.7 %collective-permute-start.7 = (bf16[2,2,96,768]{3,2,1,0:T(8,128)(2,1)}, bf16[2,2,96,768]{3,2,1,0:T(8,128)(2,1)}, u32[]{:S(2)}, u32[]{:S(2)}) collective-permute-start(bf16[2,2,96,768]{3,2,1,0:T(8,128)(2,1)} %pad_maximum_fusion.4.own), channel_id=1, source_target_pairs={{0,12},{1,13},{2,14},{3,15},{4,8},{5,9},{6,10},{7,11},{8,4},{9,5},... | collective-permute-start | bytes 1769480 | tf_op jit(solution)/shard_map/ppermute | solution.py:27
  26.6 7.5 %collective-permute-done.7.own2 = bf16[2,2,96,768]{3,2,1,0:T(8,128)(2,1)} collective-permute-done((bf16[2,2,96,768]{3,2,1,0:T(8,128)(2,1)}, bf16[2,2,96,768]{3,2,1,0:T(8,128)(2,1)}, u32[]{:S(2)}, u32[]{:S(2)}) %collective-permute-start.7) | collective-permute-done | bytes 589856 | tf_op jit(solution)/shard_map/ppermute | solution.py:27
  34.0 4.8 %collective-permute-start.9 = (bf16[2,2,96,768]{3,2,1,0:T(8,128)(2,1)}, bf16[2,2,96,768]{3,2,1,0:T(8,128)(2,1)}, u32[]{:S(2)}, u32[]{:S(2)}) collective-permute-start(bf16[2,2,96,768]{3,2,1,0:T(8,128)(2,1)} %collective-permute-done.7.own2), channel_id=1, source_target_pairs={{0,3},{1,0},{2,1},{3,2},{4,7},{5,4},{6,5},{7,6},{8,11},{9,8},{10,9... | collective-permute-start | bytes 1769480 | tf_op jit(solution)/shard_map/ppermute | solution.py:27
  38.8 4.1 %conv.2 = bf16[16,2,32,16]{3,2,1,0:T(8,128)(2,1)S(1)} custom-call(bf16[32,2,32,512]{3,2,1,0:T(8,128)(2,1)S(1)} %copy-done.2, bf16[16,2,32,512]{3,2,1,0:T(8,128)(2,1)} %collective-permute-done.before, bf16[16,2,32,512]{3,2,1,0:T(8,128)(2,1)S(1)} %fusion.9.normed, bf16[3,512,512]{2,1,0:T(8,128)(2,1)} %bitcast.96, bf16[512,16]{1,0:T(8,128)(2,1)S(1)} %copy-done.5), custom_call_target="tpu_custom_call" | custom-call | flops 1610612736 | bytes 4194304 | tf_op jit(solution)/shard_map/conv/pallas_call | solution.py:140
  43.2 4.3 %conv.3 = bf16[16,2,32,16]{3,2,1,0:T(8,128)(2,1)S(1)} custom-call(bf16[32,2,32,512]{3,2,1,0:T(8,128)(2,1)S(1)} %copy-done.2, bf16[16,2,32,512]{3,2,1,0:T(8,128)(2,1)} %collective-permute-done.2.before, bf16[16,2,32,512]{3,2,1,0:T(8,128)(2,1)} %fusion.13.normed, bf16[3,512,512]{2,1,0:T(8,128)(2,1)} %bitcast.97, bf16[512,16]{1,0:T(8,128)(2,1)S(1)} %copy-done.5), custom_call_target="tpu_custom_call" | custom-call | flops 1610612736 | bytes 4194304 | tf_op jit(solution)/shard_map/conv/pallas_call | solution.py:140
  49.5 6.1 %all-to-all-start = ((bf16[32,56,128]{2,1,0:T(8,128)(2,1)}), bf16[32,56,128]{2,1,0:T(8,128)(2,1)S(1)}, u32[]{:S(2)}, u32[]{:S(2)}) async-start(bf16[32,56,128]{2,1,0:T(8,128)(2,1)} %pad_maximum_fusion.5), calls=%async_computation | async-start | bytes 917504 | tf_op jit(solution)/shard_map/all_to_all | solution.py:353
  55.7 2.5 %collective-permute-start.5 = (bf16[2,2,96,768]{3,2,1,0:T(8,128)(2,1)}, bf16[2,2,96,768]{3,2,1,0:T(8,128)(2,1)S(1)}, u32[]{:S(2)}, u32[]{:S(2)}) collective-permute-start(bf16[2,2,96,768]{3,2,1,0:T(8,128)(2,1)} %pad_maximum_fusion.4.own), channel_id=1, source_target_pairs={{0,3},{1,0},{2,1},{3,2},{4,7},{5,4},{6,5},{7,6},{8,11},{9,8},{10,9... | collective-permute-start | bytes 1769480 | tf_op jit(solution)/shard_map/ppermute | solution.py:27
  58.2 3.5 %collective-permute-start.13 = (bf16[512,1536]{1,0:T(8,128)(2,1)}, bf16[512,1536]{1,0:T(8,128)(2,1)}, u32[]{:S(2)}, u32[]{:S(2)}) collective-permute-start(bf16[512,1536]{1,0:T(8,128)(2,1)} %bitcast.15.x), channel_id=1, source_target_pairs={{0,32},{32,0},{1,33},{33,1},{2,34},{34,2},{3,35},{35,3},{4,36},{36... | collective-permute-start | bytes 4718600 | tf_op jit(solution)/shard_map/ppermute | solution.py:45
  67.7 4.4 %shard_map.130 = (bf16[512,3072]{1,0:T(8,128)(2,1)}, bf16[512,1536]{1,0:T(8,128)(2,1)S(1)}, bf16[512,1536]{1,0:T(8,128)(2,1)}) custom-call(s32[1]{0:T(128)} %bitcast.idx, bf16[512,64]{1,0:T(8,128)(2,1)S(1)} %bitcast.92, bf16[3072,64]{1,0:T(8,128)(2,1)S(1)} %bitcast.90, f32[1,3072]{1,0:T(1,128)S(1)} %copy-done.8, f32[1,3072]{1,0:T(1,128)S(1)} %copy-done.9), custom_call_target="tpu_custom_call" | custom-call | flops 1610612736 | bytes 16777216 | tf_op jit(solution)/shard_map/pallas_call | solution.py:331
  73.3 4.6 %collective-permute-start.12 = (bf16[512,1536]{1,0:T(8,128)(2,1)}, bf16[512,1536]{1,0:T(8,128)(2,1)}, u32[]{:S(2)}, u32[]{:S(2)}) collective-permute-start(bf16[512,1536]{1,0:T(8,128)(2,1)} %get-tuple-element.25), channel_id=1, source_target_pairs={{0,32},{32,0},{1,33},{33,1},{2,34},{34,2},{3,35},{35,3},{4,36},{36... | collective-permute-start | bytes 4718600 | tf_op jit(solution)/shard_map/ppermute | solution.py:45
  78.5 6.8 %place.1 = bf16[2,4,4,96,768]{4,3,2,1,0:T(8,128)(2,1)} custom-call(s32[4]{0:T(128)S(1)} %pad_add_fusion.idx, bf16[2,2,96,768]{3,2,1,0:T(8,128)(2,1)} %pad_maximum_fusion.4.own, bf16[2,2,96,768]{3,2,1,0:T(8,128)(2,1)} %collective-permute-done.4.up, bf16[2,2,96,768]{3,2,1,0:T(8,128)(2,1)S(1)} %collective-permute-done.5.down, ...), custom_call_target="tpu_custom_call" | custom-call | bytes 9437184 | tf_op jit(solution)/shard_map/place/pallas_call | solution.py:86
  87.4 4.0 %flip.1.cot_t = bf16[1536,512]{1,0:T(8,128)(2,1)} custom-call(bf16[512,1536]{1,0:T(8,128)(2,1)} %bitcast.15.x), custom_call_target="tpu_custom_call" | custom-call | bytes 3145728 | tf_op jit(solution)/shard_map/flip/pallas_call | solution.py:109
  91.4 7.3 %convolution_convert_fusion = bf16[1536,1536]{1,0:T(8,128)(2,1)S(1)} fusion(bf16[512,1536]{1,0:T(8,128)(2,1)} %collective-permute-done.12, bf16[512,1536]{1,0:T(8,128)(2,1)S(1)} %copy-done.11, bf16[512,1536]{1,0:T(8,128)(2,1)} %collective-permute-done.13, bf16[512,1536]{1,0:T(8,128)(2,1)} %bitcast.15.x), kind=kOutput, calls=%fused_computation.1 | convolution fusion | flops 4846780416 | bytes 11010048 | tf_op jit(solution)/shard_map/dot_general | solution.py:513
  103.6 2.7 %collective-permute-start.15 = (bf16[4,96,1536]{2,1,0:T(8,128)(2,1)}, bf16[4,96,1536]{2,1,0:T(8,128)(2,1)}, u32[]{:S(2)}, u32[]{:S(2)}) collective-permute-start(bf16[4,96,1536]{2,1,0:T(8,128)(2,1)} %pad_maximum_fusion.2), channel_id=1, source_target_pairs={{0,12},{1,13},{2,14},{3,15},{4,0},{5,1},{6,2},{7,3},{8,4},{9,5},{1... | collective-permute-start | bytes 3538952 | tf_op jit(solution)/shard_map/ppermute | solution.py:27
  108.0 13.3 %backward.1 = f32[3072,64]{1,0:T(8,128)S(1)} custom-call(s32[1]{0:T(128)} %bitcast.idx, bf16[64,512]{1,0:T(8,128)(2,1)S(1)} %copy.30.tok_t, bf16[512,64]{1,0:T(8,128)(2,1)S(1)} %bitcast.94, bf16[3072,64]{1,0:T(8,128)(2,1)S(1)} %bitcast.91, f32[3072,128]{1,0:T(8,128)S(1)} %broadcast_in_dim.35.scaling, bf16[1536,512]{1,0:T(8,128)(2,1)S(1)} %copy-done.4, ...), custom_call_target="tpu_custom_call" | custom-call | flops 4831838208 | bytes 16777216 | tf_op jit(solution)/shard_map/backward/pallas_call | solution.py:254
  124.5 2.4 %add_convert_fusion.3 = bf16[2,96,1536]{2,1,0:T(8,128)(2,1)} fusion(bf16[4,96,1536]{2,1,0:T(8,128)(2,1)} %copy-done.15, bf16[4,96,1536]{2,1,0:T(8,128)(2,1)} %collective-permute-done.14), kind=kLoop, calls=%fused_computation.30 | loop fusion | flops 1179648 | bytes 1769472 | tf_op jit(solution)/shard_map/convert_element_type | solution.py:379
  128.9 2.7 %collective-permute-start.18 = (bf16[2,96,1536]{2,1,0:T(8,128)(2,1)}, bf16[2,96,1536]{2,1,0:T(8,128)(2,1)}, u32[]{:S(2)}, u32[]{:S(2)}) collective-permute-start(bf16[2,96,1536]{2,1,0:T(8,128)(2,1)} %add_convert_fusion.2), channel_id=1, source_target_pairs={{0,12},{1,13},{2,14},{3,15},{4,0},{5,1},{6,2},{7,3},{8,4},{9,5},{1... | collective-permute-start | bytes 1769480 | tf_op jit(solution)/shard_map/ppermute | solution.py:27
  135.8 2.6 %collective-permute-done.21 = bf16[4,96,64]{2,1,0:T(8,128)(2,1)S(1)} collective-permute-done((bf16[4,96,64]{2,1,0:T(8,128)(2,1)S(1)}, bf16[4,96,64]{2,1,0:T(8,128)(2,1)S(1)}, u32[]{:S(2)}, u32[]{:S(2)}) %collective-permute-start.21) | collective-permute-done | bytes 49184 | tf_op jit(solution)/shard_map/ppermute | solution.py:27
  138.4 2.8 %collective-permute-done.20 = bf16[4,96,64]{2,1,0:T(8,128)(2,1)S(1)} collective-permute-done((bf16[4,96,64]{2,1,0:T(8,128)(2,1)S(1)}, bf16[4,96,64]{2,1,0:T(8,128)(2,1)S(1)}, u32[]{:S(2)}, u32[]{:S(2)}) %collective-permute-start.20) | collective-permute-done | bytes 49184 | tf_op jit(solution)/shard_map/ppermute | solution.py:27
  148.0 5.6 %values.2.rest_0_ = bf16[512,1536]{1,0:T(8,128)(2,1)} custom-call(s32[1]{0:T(128)} %bitcast.idx, bf16[512,3072]{1,0:T(8,128)(2,1)S(1)} %copy-done.3, bf16[3072,768]{1,0:T(8,128)(2,1)} %bitcast.13.weight.w_kept), custom_call_target="tpu_custom_call" | custom-call | flops 2415919104 | bytes 7340032 | tf_op jit(solution)/shard_map/values/pallas_call | solution.py:298
  160.2 5.6 %values.3 = bf16[512,1536]{1,0:T(8,128)(2,1)} custom-call(s32[1]{0:T(128)S(6)} %sub.27.idx, bf16[512,3072]{1,0:T(8,128)(2,1)S(1)} %copy-done.3, bf16[3072,768]{1,0:T(8,128)(2,1)} %collective-permute-done.11.weight.w_got, bf16[512,1536]{1,0:T(8,128)(2,1)} %values.2.rest_0_), custom_call_target="tpu_custom_call", output_to_operand_aliasing={{}: (3, {})} | custom-call | flops 2415919104 | bytes 7340032 | tf_op jit(solution)/shard_map/values/pallas_call | solution.py:298
  165.8 2.2 %collective-permute-done.25 = f32[24,1600]{1,0:T(8,128)S(1)} collective-permute-done((f32[24,1600]{1,0:T(8,128)S(1)}, f32[24,1600]{1,0:T(8,128)S(1)}, u32[]{:S(2)}, u32[]{:S(2)}) %collective-permute-start.25) | collective-permute-done | bytes 153632 | tf_op jit(solution)/shard_map/ppermute | solution.py:27
  (149 shorter events, 58.9 us)
Async XLA Ops:
  2.3 12.1 %collective-permute-start.1 = (bf16[96,768]{1,0:T(8,128)(2,1)}, bf16[96,768]{1,0:T(8,128)(2,1)}, u32[]{:S(2)}, u32[]{:S(2)}) collective-permute-start(bf16[96,768]{1,0:T(8,128)(2,1)} %constant_dynamic-slice_fusion), channel_id=1, source_target_pairs={{0,80},{1,81},{2,82},{3,83},{4,84},{5,85},{6,86},{7,87},{8,88},{9,... | collective-permute-start | bytes 442376 | tf_op jit(solution)/shard_map/ppermute | solution.py:27
  11.0 27.7 %collective-permute-start = (bf16[16,2,32,512]{3,2,1,0:T(8,128)(2,1)S(1)}, bf16[16,2,32,512]{3,2,1,0:T(8,128)(2,1)}, u32[]{:S(2)}, u32[]{:S(2)}) collective-permute-start(bf16[16,2,32,512]{3,2,1,0:T(8,128)(2,1)S(1)} %fusion.9.normed), channel_id=1, source_target_pairs={{0,32},{32,64},{64,96},{1,33},{33,65},{65,97},{2,34},{34,66},{66,9... | collective-permute-start | bytes 3145736 | tf_op jit(solution)/shard_map/ppermute | solution.py:456
  18.4 24.8 %collective-permute-start.2 = (bf16[16,2,32,512]{3,2,1,0:T(8,128)(2,1)}, bf16[16,2,32,512]{3,2,1,0:T(8,128)(2,1)}, u32[]{:S(2)}, u32[]{:S(2)}) collective-permute-start(bf16[16,2,32,512]{3,2,1,0:T(8,128)(2,1)} %fusion.13.normed), channel_id=1, source_target_pairs={{0,32},{32,64},{64,96},{1,33},{33,65},{65,97},{2,34},{34,66},{66,9... | collective-permute-start | bytes 3145736 | tf_op jit(solution)/shard_map/ppermute | solution.py:456
  22.4 11.6 %collective-permute-start.7 = (bf16[2,2,96,768]{3,2,1,0:T(8,128)(2,1)}, bf16[2,2,96,768]{3,2,1,0:T(8,128)(2,1)}, u32[]{:S(2)}, u32[]{:S(2)}) collective-permute-start(bf16[2,2,96,768]{3,2,1,0:T(8,128)(2,1)} %pad_maximum_fusion.4.own), channel_id=1, source_target_pairs={{0,12},{1,13},{2,14},{3,15},{4,8},{5,9},{6,10},{7,11},{8,4},{9,5},... | collective-permute-start | bytes 1769480 | tf_op jit(solution)/shard_map/ppermute | solution.py:27
  25.3 37.6 %collective-permute-start.4 = (bf16[2,2,96,768]{3,2,1,0:T(8,128)(2,1)}, bf16[2,2,96,768]{3,2,1,0:T(8,128)(2,1)}, u32[]{:S(2)}, u32[]{:S(2)}) collective-permute-start(bf16[2,2,96,768]{3,2,1,0:T(8,128)(2,1)} %pad_maximum_fusion.4.own), channel_id=1, source_target_pairs={{0,1},{1,2},{2,3},{3,0},{4,5},{5,6},{6,7},{7,4},{8,9},{9,10},{10,1... | collective-permute-start | bytes 1769480 | tf_op jit(solution)/shard_map/ppermute | solution.py:27
  34.0 30.1 %collective-permute-start.9 = (bf16[2,2,96,768]{3,2,1,0:T(8,128)(2,1)}, bf16[2,2,96,768]{3,2,1,0:T(8,128)(2,1)}, u32[]{:S(2)}, u32[]{:S(2)}) collective-permute-start(bf16[2,2,96,768]{3,2,1,0:T(8,128)(2,1)} %collective-permute-done.7.own2), channel_id=1, source_target_pairs={{0,3},{1,0},{2,1},{3,2},{4,7},{5,4},{6,5},{7,6},{8,11},{9,8},{10,9... | collective-permute-start | bytes 1769480 | tf_op jit(solution)/shard_map/ppermute | solution.py:27
  49.5 16.4 %all-to-all-start = ((bf16[32,56,128]{2,1,0:T(8,128)(2,1)}), bf16[32,56,128]{2,1,0:T(8,128)(2,1)S(1)}, u32[]{:S(2)}, u32[]{:S(2)}) async-start(bf16[32,56,128]{2,1,0:T(8,128)(2,1)} %pad_maximum_fusion.5), calls=%async_computation | async-start | bytes 917504 | tf_op jit(solution)/shard_map/all_to_all | solution.py:353
  55.7 17.6 %collective-permute-start.5 = (bf16[2,2,96,768]{3,2,1,0:T(8,128)(2,1)}, bf16[2,2,96,768]{3,2,1,0:T(8,128)(2,1)S(1)}, u32[]{:S(2)}, u32[]{:S(2)}) collective-permute-start(bf16[2,2,96,768]{3,2,1,0:T(8,128)(2,1)} %pad_maximum_fusion.4.own), channel_id=1, source_target_pairs={{0,3},{1,0},{2,1},{3,2},{4,7},{5,4},{6,5},{7,6},{8,11},{9,8},{10,9... | collective-permute-start | bytes 1769480 | tf_op jit(solution)/shard_map/ppermute | solution.py:27
  58.2 33.2 %collective-permute-start.13 = (bf16[512,1536]{1,0:T(8,128)(2,1)}, bf16[512,1536]{1,0:T(8,128)(2,1)}, u32[]{:S(2)}, u32[]{:S(2)}) collective-permute-start(bf16[512,1536]{1,0:T(8,128)(2,1)} %bitcast.15.x), channel_id=1, source_target_pairs={{0,32},{32,0},{1,33},{33,1},{2,34},{34,2},{3,35},{35,3},{4,36},{36... | collective-permute-start | bytes 4718600 | tf_op jit(solution)/shard_map/ppermute | solution.py:45
  61.7 16.8 %collective-permute-start.8 = (bf16[2,2,96,768]{3,2,1,0:T(8,128)(2,1)}, bf16[2,2,96,768]{3,2,1,0:T(8,128)(2,1)S(1)}, u32[]{:S(2)}, u32[]{:S(2)}) collective-permute-start(bf16[2,2,96,768]{3,2,1,0:T(8,128)(2,1)} %collective-permute-done.7.own2), channel_id=1, source_target_pairs={{0,1},{1,2},{2,3},{3,0},{4,5},{5,6},{6,7},{7,4},{8,9},{9,10},{10,1... | collective-permute-start | bytes 1769480 | tf_op jit(solution)/shard_map/ppermute | solution.py:27
  62.9 15.6 %collective-permute-start.6 = (bf16[2,2,96,768]{3,2,1,0:T(8,128)(2,1)}, bf16[2,2,96,768]{3,2,1,0:T(8,128)(2,1)S(1)}, u32[]{:S(2)}, u32[]{:S(2)}) collective-permute-start(bf16[2,2,96,768]{3,2,1,0:T(8,128)(2,1)} %collective-permute-done.4.up), channel_id=1, source_target_pairs={{0,1},{1,2},{2,3},{3,0},{4,5},{5,6},{6,7},{7,4},{8,9},{9,10},{10,1... | collective-permute-start | bytes 1769480 | tf_op jit(solution)/shard_map/ppermute | solution.py:27
  64.1 14.4 %collective-permute-start.10 = (bf16[2,2,96,768]{3,2,1,0:T(8,128)(2,1)}, bf16[2,2,96,768]{3,2,1,0:T(8,128)(2,1)S(1)}, u32[]{:S(2)}, u32[]{:S(2)}) collective-permute-start(bf16[2,2,96,768]{3,2,1,0:T(8,128)(2,1)} %collective-permute-done.9.down2), channel_id=1, source_target_pairs={{0,3},{1,0},{2,1},{3,2},{4,7},{5,4},{6,5},{7,6},{8,11},{9,8},{10,9... | collective-permute-start | bytes 1769480 | tf_op jit(solution)/shard_map/ppermute | solution.py:27
  73.3 18.1 %collective-permute-start.12 = (bf16[512,1536]{1,0:T(8,128)(2,1)}, bf16[512,1536]{1,0:T(8,128)(2,1)}, u32[]{:S(2)}, u32[]{:S(2)}) collective-permute-start(bf16[512,1536]{1,0:T(8,128)(2,1)} %get-tuple-element.25), channel_id=1, source_target_pairs={{0,32},{32,0},{1,33},{33,1},{2,34},{34,2},{3,35},{35,3},{4,36},{36... | collective-permute-start | bytes 4718600 | tf_op jit(solution)/shard_map/ppermute | solution.py:45
  85.3 21.1 %collective-permute-start.11 = (bf16[3072,768]{1,0:T(8,128)(2,1)}, bf16[3072,768]{1,0:T(8,128)(2,1)}, u32[]{:S(2)}, u32[]{:S(2)}) collective-permute-start(bf16[3072,768]{1,0:T(8,128)(2,1)} %bitcast.13.weight.w_kept), channel_id=1, source_target_pairs={{0,32},{32,0},{1,33},{33,1},{2,34},{34,2},{3,35},{35,3},{4,36},{36... | collective-permute-start | bytes 14155784 | tf_op jit(solution)/shard_map/ppermute | solution.py:45
  102.4 20.5 %collective-permute-start.14 = (bf16[4,96,1536]{2,1,0:T(8,128)(2,1)}, bf16[4,96,1536]{2,1,0:T(8,128)(2,1)}, u32[]{:S(2)}, u32[]{:S(2)}) collective-permute-start(bf16[4,96,1536]{2,1,0:T(8,128)(2,1)} %pad_maximum_fusion.1), channel_id=1, source_target_pairs={{0,4},{1,5},{2,6},{3,7},{4,8},{5,9},{6,10},{7,11},{8,12},{9,13},{1... | collective-permute-start | bytes 3538952 | tf_op jit(solution)/shard_map/ppermute | solution.py:27
  103.6 19.3 %collective-permute-start.15 = (bf16[4,96,1536]{2,1,0:T(8,128)(2,1)}, bf16[4,96,1536]{2,1,0:T(8,128)(2,1)}, u32[]{:S(2)}, u32[]{:S(2)}) collective-permute-start(bf16[4,96,1536]{2,1,0:T(8,128)(2,1)} %pad_maximum_fusion.2), channel_id=1, source_target_pairs={{0,12},{1,13},{2,14},{3,15},{4,0},{5,1},{6,2},{7,3},{8,4},{9,5},{1... | collective-permute-start | bytes 3538952 | tf_op jit(solution)/shard_map/ppermute | solution.py:27
  126.8 14.5 %collective-permute-start.17 = (bf16[2,96,1536]{2,1,0:T(8,128)(2,1)}, bf16[2,96,1536]{2,1,0:T(8,128)(2,1)}, u32[]{:S(2)}, u32[]{:S(2)}) collective-permute-start(bf16[2,96,1536]{2,1,0:T(8,128)(2,1)} %add_convert_fusion.3), channel_id=1, source_target_pairs={{0,4},{1,5},{2,6},{3,7},{4,8},{5,9},{6,10},{7,11},{8,12},{9,13},{1... | collective-permute-start | bytes 1769480 | tf_op jit(solution)/shard_map/ppermute | solution.py:27
  128.9 12.5 %collective-permute-start.18 = (bf16[2,96,1536]{2,1,0:T(8,128)(2,1)}, bf16[2,96,1536]{2,1,0:T(8,128)(2,1)}, u32[]{:S(2)}, u32[]{:S(2)}) collective-permute-start(bf16[2,96,1536]{2,1,0:T(8,128)(2,1)} %add_convert_fusion.2), channel_id=1, source_target_pairs={{0,12},{1,13},{2,14},{3,15},{4,0},{5,1},{6,2},{7,3},{8,4},{9,5},{1... | collective-permute-start | bytes 1769480 | tf_op jit(solution)/shard_map/ppermute | solution.py:27
  145.5 8.0 %collective-permute-start.24 = (bf16[96,1600]{1,0:T(8,128)(2,1)}, bf16[96,1600]{1,0:T(8,128)(2,1)}, u32[]{:S(2)}, u32[]{:S(2)}) collective-permute-start(bf16[96,1600]{1,0:T(8,128)(2,1)} %get-tuple-element.42), channel_id=1, source_target_pairs={{0,16},{1,17},{2,18},{3,19},{4,20},{5,21},{6,22},{7,23},{8,24},{9,... | collective-permute-start | bytes 921608 | tf_op jit(solution)/shard_map/ppermute | solution.py:27
  146.5 8.8 %collective-permute-start.23 = (bf16[96,1600]{1,0:T(8,128)(2,1)}, bf16[96,1600]{1,0:T(8,128)(2,1)}, u32[]{:S(2)}, u32[]{:S(2)}) collective-permute-start(bf16[96,1600]{1,0:T(8,128)(2,1)} %get-tuple-element.43), channel_id=1, source_target_pairs={{0,80},{1,81},{2,82},{3,83},{4,84},{5,85},{6,86},{7,87},{8,88},{9,... | collective-permute-start | bytes 921608 | tf_op jit(solution)/shard_map/ppermute | solution.py:27
  147.7 9.2 %collective-permute-start.22 = (bf16[96,1600]{1,0:T(8,128)(2,1)}, bf16[96,1600]{1,0:T(8,128)(2,1)}, u32[]{:S(2)}, u32[]{:S(2)}) collective-permute-start(bf16[96,1600]{1,0:T(8,128)(2,1)} %get-tuple-element.41), channel_id=1, source_target_pairs={{0,64},{1,65},{2,66},{3,67},{4,68},{5,69},{6,70},{7,71},{8,72},{9,... | collective-permute-start | bytes 921608 | tf_op jit(solution)/shard_map/ppermute | solution.py:27
  158.4 7.5 %collective-permute-start.27 = (f32[24,1600]{1,0:T(8,128)S(1)}, f32[24,1600]{1,0:T(8,128)S(1)}, u32[]{:S(2)}, u32[]{:S(2)}) collective-permute-start(f32[24,1600]{1,0:T(8,128)S(1)} %get-tuple-element.49), channel_id=1, source_target_pairs={{0,2},{1,3},{2,0},{3,1},{4,6},{5,7},{6,4},{7,5},{8,10},{9,11},{10,... | collective-permute-start | bytes 460808 | tf_op jit(solution)/shard_map/ppermute | solution.py:27
  158.7 7.1 %collective-permute-start.26 = (f32[24,1600]{1,0:T(8,128)S(1)}, f32[24,1600]{1,0:T(8,128)S(1)}, u32[]{:S(2)}, u32[]{:S(2)}) collective-permute-start(f32[24,1600]{1,0:T(8,128)S(1)} %get-tuple-element.50), channel_id=1, source_target_pairs={{0,3},{1,0},{2,1},{3,2},{4,7},{5,4},{6,5},{7,6},{8,11},{9,8},{10,9... | collective-permute-start | bytes 460808 | tf_op jit(solution)/shard_map/ppermute | solution.py:27
  159.9 8.2 %collective-permute-start.25 = (f32[24,1600]{1,0:T(8,128)S(1)}, f32[24,1600]{1,0:T(8,128)S(1)}, u32[]{:S(2)}, u32[]{:S(2)}) collective-permute-start(f32[24,1600]{1,0:T(8,128)S(1)} %get-tuple-element.51), channel_id=1, source_target_pairs={{0,1},{1,2},{2,3},{3,0},{4,5},{5,6},{6,7},{7,4},{8,9},{9,10},{10,1... | collective-permute-start | bytes 460808 | tf_op jit(solution)/shard_map/ppermute | solution.py:27
  (29 other events, 169.2 us)
